TPU v7x, 32 devices: a whole 2x2x4 slice. The times are simulated.
32 devices in a mesh: rows: 8 (over y, x, core), grp: 4 (over z).
Axes of the slice: x: 2, y: 2, z: 4, core: 2. Of those that a mesh axis runs over, the one named last changes fastest.
Arguments:
- pivot_columns: bfloat16 [32, 10240, 256], P('rows', 'grp'), may hold values from -6 to 6
- previous: bfloat16 [32, 10240, 512], P('rows', 'grp'), may hold values from -0.59765625 to 0.59765625
- pivots: int32 [256], replicated, may hold values from 0 to 327679, as said below
- pivot_inverse: bfloat16 [256, 256], replicated, may hold values from -0.4 to 1.5
- orbitals: bfloat16 [10240, 1024], P('grp'), may hold values from -0.0625 to 0.0625
- slab_orbitals: bfloat16 [32, 1024], replicated, may hold values from -1 to 1
Outputs:
- new_vectors: bfloat16 [32, 10240, 256], P('rows', 'grp')
- mo_block: bfloat16 [256, 1024, 1024], P('rows', None, 'grp')
Inputs may be any that keep to these rules, and one draw needn't show every extreme that they name: `pivots`: distinct entries.
All inputs are finite; a program needn't handle non-finite values.
Results may differ from a plain program's by a relative error of at most 0.0038.
The roundings to bfloat16 on the way count: a program that leaves them out, or rounds other values in their place, can miss the bound.
Values may be sent and summed in bfloat16 or wider, within the bound.
A program may use at most 128 MiB of HBM per device.

v0:
```python
import functools

import jax
import jax.numpy as jnp
from jax import lax
from jax.experimental import pallas as pl
from jax.experimental.pallas import tpu as pltpu
from jax.sharding import PartitionSpec as P

F32 = jnp.float32
BF16 = jnp.bfloat16
MESH = pl.DeviceIdType.MESH


def relayed(G):
    return G >= 4


def fused_kernel(
    R, G, x_ref, pc_hbm, prev_hbm, inv_ref, orb_hbm, out_hbm, new_hbm,
    buf_a, buf_b, buf_c, rows_wide, rows_v, upper_v, new_v, prev_v, orb_v, turned, block_v, send, relay,
    send_a, recv_a, send_b, recv_b, send_c, recv_c, in_sem, new_sem, own_sem, send_sem, recv_sem, relay_sem,
):
    r = lax.axis_index("rows")
    g = lax.axis_index("grp")
    N = R * G
    me = r * G + g
    mu_dev, nu, p = new_v.shape
    _, _, _, pl_dev, j_dev = send.shape
    c = buf_c.shape[1]

    def load(mu):
        return (
            pltpu.make_async_copy(prev_hbm.at[mu], prev_v.at[mu], in_sem.at[2 * mu]),
            pltpu.make_async_copy(pc_hbm.at[mu], new_v.at[mu], in_sem.at[2 * mu + 1]),
        )

    load_orb = pltpu.make_async_copy(orb_hbm, orb_v, in_sem.at[2 * mu_dev])
    for mu in range(mu_dev):
        for copy in load(mu):
            copy.start()
        if mu == 0:
            load_orb.start()

    barrier = pltpu.get_barrier_semaphore()

    @pl.loop(1, N)
    def _(d):
        peer = lax.rem(me + d, N)
        pl.semaphore_signal(
            barrier, inc=1, device_id={"rows": peer // G, "grp": lax.rem(peer, G)}, device_id_type=MESH
        )

    shape = (p, p)
    low = lax.broadcasted_iota(jnp.int32, shape, 0)
    high = lax.broadcasted_iota(jnp.int32, shape, 1)
    upper_v[...] = jnp.where(low <= high, inv_ref[...].astype(F32), 0.0).astype(BF16)
    pl.semaphore_wait(barrier, N - 1)

    def remote(src, dst, send, recv, row, grp):
        return pltpu.make_async_remote_copy(
            src_ref=src, dst_ref=dst, send_sem=send, recv_sem=recv,
            device_id={"rows": row, "grp": grp}, device_id_type=MESH,
        )

    row_peers = [(d, lax.rem(r + d, R)) for d in range(1, R)]
    grp_peers = [(d, lax.rem(g + d, G)) for d in range(1, G)]
    first = [remote(x_ref.at[q], buf_a.at[d], send_a.at[d], recv_a.at[d], q, g) for d, q in row_peers]
    for copy in first:
        copy.start()
    total = x_ref[r].astype(F32)
    for (d, _), copy in zip(row_peers, first):
        copy.wait_recv()
        total = total + buf_a[d].astype(F32)
    buf_b[0] = total.astype(BF16)
    second = [remote(buf_b.at[0], buf_b.at[d], send_b.at[d], recv_b.at[d], r, q) for d, q in grp_peers]
    for copy in second:
        copy.start()
    for (d, _), copy in zip(grp_peers, second):
        copy.wait_recv()
        total = total + buf_b[d].astype(F32)
    buf_c[r] = total.astype(BF16)
    third = [remote(buf_c.at[r], buf_c.at[r], send_c.at[d], recv_c.at[d], q, g) for d, q in row_peers]
    for copy in third:
        copy.start()
    for copy in third:
        copy.wait_recv()
    for copy in first + second + third:
        copy.wait_send()
    for k in range(R):
        rows_wide[k * c : (k + 1) * c, :] = buf_c[k].astype(F32)
    rows_v[...] = rows_wide[...].astype(BF16)
    load_orb.wait()

    chunk = 512 if nu % 512 == 0 else 256
    edge = (g == 0) | (g == G - 1)
    across = G - 1 - g
    falling = (g == 0) | ((2 * g >= G) & (g != G - 1))

    def store_new(mu):
        return pltpu.make_async_copy(new_v.at[mu], new_hbm.at[mu], new_sem.at[mu])

    @pl.loop(0, mu_dev)
    def _(mu):
        for copy in load(mu):
            copy.wait()
        eye = jnp.where(
            lax.broadcasted_iota(jnp.int32, shape, 0) == lax.broadcasted_iota(jnp.int32, shape, 1), 1.0, 0.0
        ).astype(BF16)

        @pl.loop(0, nu // chunk)
        def _(i):
            at = pl.ds(pl.multiple_of(i * chunk, chunk), chunk)
            correction = lax.dot_general(
                prev_v[mu, at, :], rows_v[...], (((1,), (1,)), ((), ())), preferred_element_type=F32
            )
            residual = (new_v[mu, at, :].astype(F32) - correction).astype(BF16)
            made = jnp.dot(residual, upper_v[...], preferred_element_type=F32).astype(BF16)
            new_v[mu, at, :] = made
            turned[:, at] = lax.dot_general(
                eye, made, (((1,), (1,)), ((), ())), preferred_element_type=F32
            ).astype(BF16)

        store_new(mu).start()
        slot = (g * R + r) * mu_dev + mu

        @pl.loop(0, G)
        def _(d):
            to = jnp.where(falling, G - 1 - d, d)
            cols = pl.ds(pl.multiple_of(to * j_dev, j_dev), j_dev)
            block_v[...] = jnp.dot(turned[...], orb_v[:, cols], preferred_element_type=F32)

            def deliver():
                for k in range(R):
                    peer = lax.rem(r + k, R)
                    src = send.at[mu, to, peer]
                    dst = out_hbm.at[slot]

                    def away():
                        remote(src, dst, send_sem, recv_sem, peer, to).start()

                    if k:
                        away()
                    else:
                        pl.when(to != g)(away)

                        @pl.when(to == g)
                        def _():
                            pltpu.make_async_copy(src, dst, own_sem).start()

            def keep():
                for k in range(R):
                    send[mu, to, k] = block_v[k * pl_dev : (k + 1) * pl_dev, :].astype(BF16)

            if not relayed(G):
                keep()
                deliver()
                return
            adds = ((g == 1) & (to == G - 1)) | ((g == G - 2) & (to == 0))
            hands = edge & (to == across)

            @pl.when(adds)
            def _():
                pltpu.make_async_copy(relay.at[mu], relay.at[mu], relay_sem.at[mu]).wait()
                for k in range(R):
                    mine = block_v[k * pl_dev : (k + 1) * pl_dev, :]
                    send[mu, to, k] = (mine + relay[mu, k].astype(F32)).astype(BF16)

            pl.when(jnp.logical_not(adds))(keep)

            @pl.when(hands)
            def _():
                via = jnp.where(g == 0, 1, G - 2)
                remote(send.at[mu, to], relay.at[mu], send_sem, relay_sem.at[mu], r, via).start()

            pl.when(jnp.logical_not(hands))(deliver)

    own = out_hbm.at[pl.ds(0, mu_dev)]
    pltpu.make_async_copy(own, own, own_sem).wait()
    for mu in range(mu_dev):
        store_new(mu).wait()
    every = out_hbm.at[pl.ds(0, (N - 1) * mu_dev)]
    pltpu.make_async_copy(every, every, send_sem).wait()
    if relayed(G):
        @pl.when(edge)
        def _():
            fewer = out_hbm.at[pl.ds(0, (N - R - 1) * mu_dev)]
            pltpu.make_async_copy(fewer, fewer, recv_sem).wait()

        @pl.when(jnp.logical_not(edge))
        def _():
            pltpu.make_async_copy(every, every, recv_sem).wait()
    else:
        pltpu.make_async_copy(every, every, recv_sem).wait()


def fused(picked, columns, previous, inverse, orbitals, R, G):
    mu_dev, nu, p = columns.shape
    k = previous.shape[2]
    c = p // R
    nj = orbitals.shape[1]
    hbm = pl.BlockSpec(memory_space=pl.ANY)
    vmem = pl.BlockSpec(memory_space=pltpu.VMEM)
    dma = pltpu.SemaphoreType.DMA
    return pl.pallas_call(
        functools.partial(fused_kernel, R, G),
        out_shape=(
            jax.ShapeDtypeStruct((R * G * mu_dev, c, nj // G), BF16),
            jax.ShapeDtypeStruct(columns.shape, BF16),
        ),
        in_specs=[vmem, hbm, hbm, vmem, hbm],
        out_specs=(hbm, hbm),
        scratch_shapes=[
            pltpu.VMEM((R, c, k), BF16),
            pltpu.VMEM((G, c, k), BF16),
            pltpu.VMEM((R, c, k), BF16),
            pltpu.VMEM((p, k), F32),
            pltpu.VMEM((p, k), BF16),
            pltpu.VMEM((p, p), BF16),
            pltpu.VMEM((mu_dev, nu, p), BF16),
            pltpu.VMEM((mu_dev, nu, k), BF16),
            pltpu.VMEM((nu, nj), BF16),
            pltpu.VMEM((p, nu), BF16),
            pltpu.VMEM((p, nj // G), F32),
            pltpu.VMEM((mu_dev, G, R, c, nj // G), BF16),
            pltpu.VMEM((mu_dev, R, c, nj // G), BF16),
            dma((R,)), dma((R,)), dma((G,)), dma((G,)), dma((R,)), dma((R,)),
            dma((2 * mu_dev + 1,)), dma((mu_dev,)), dma(()), dma(()), dma(()), dma((mu_dev,)),
        ],
        compiler_params=pltpu.CompilerParams(
            collective_id=0, has_side_effects=True, vmem_limit_bytes=60 * 1024 * 1024
        ),
        name="fused_exchange",
    )(picked, columns, previous, inverse, orbitals)


def block_kernel(part_ref, slab_ref, out_ref, half_ref, sorted_ref, slab_t_ref):
    groups, rows, _ = part_ref.shape
    mus = slab_ref.shape[0]
    block = out_ref.shape[0]
    vecs = rows // mus
    step = pl.program_id(0)
    g = lax.axis_index("grp")

    @pl.when(step == 0)
    def _():
        slab_t_ref[...] = slab_ref[...].astype(F32).T.astype(BF16)
        piece = 128

        @pl.loop(0, rows // piece)
        def _(i):
            at = pl.ds(pl.multiple_of(i * piece, piece), piece)
            total = jnp.zeros((piece, part_ref.shape[2]), F32)
            for k in range(groups):
                part = part_ref[k, at, :].astype(F32)
                if relayed(groups) and k in (0, groups - 1):
                    part = jnp.where(g == groups - 1 - k, 0.0, part)
                total = total + part
            half_ref[at, :] = total.astype(BF16)

        shift = mus.bit_length() - 1

        @pl.loop(0, rows // piece)
        def _(i):
            at = pl.ds(pl.multiple_of(i * piece, piece), piece)
            row = lax.broadcasted_iota(jnp.int32, (piece, rows), 0) + i * piece
            col = lax.broadcasted_iota(jnp.int32, (piece, rows), 1)
            source = (row & (mus - 1)) * vecs + lax.shift_right_logical(row, shift)
            pick = jnp.where(source == col, 1.0, 0.0).astype(BF16)
            sorted_ref[at, :] = jnp.dot(pick, half_ref[...], preferred_element_type=F32).astype(BF16)

    for q in range(block):
        at = pl.ds(pl.multiple_of((step * block + q) * mus, mus), mus)
        out_ref[q] = jnp.dot(slab_t_ref[...], sorted_ref[at, :], preferred_element_type=F32).astype(BF16)


def orbital_block(parts, slab):
    groups, rows, j = parts.shape
    mus, i = slab.shape
    assert mus & (mus - 1) == 0
    vecs = rows // mus
    block = 4 if vecs % 4 == 0 else 1
    return pl.pallas_call(
        block_kernel,
        grid=(vecs // block,),
        out_shape=jax.ShapeDtypeStruct((vecs, i, j), BF16),
        in_specs=[
            pl.BlockSpec((groups, rows, j), lambda s: (0, 0, 0)),
            pl.BlockSpec((mus, i), lambda s: (0, 0)),
        ],
        out_specs=pl.BlockSpec((block, i, j), lambda s: (s, 0, 0)),
        scratch_shapes=[
            pltpu.VMEM((rows, j), BF16),
            pltpu.VMEM((rows, j), BF16),
            pltpu.VMEM((i, mus), BF16),
        ],
        name="orbital_block",
    )(parts, slab)


def per_device(R, G, pivot_columns, previous, pivots, pivot_inverse, orbitals, slab_orbitals):
    mu_dev, nu_dev, prev_count = previous.shape
    count = pivot_columns.shape[2]
    nbas = nu_dev * G
    row_index = lax.axis_index("rows")
    grp_index = lax.axis_index("grp")
    first_local = pivots // nbas - row_index * mu_dev
    second_local = pivots % nbas - grp_index * nu_dev
    owned = (
        (first_local >= 0) & (first_local < mu_dev) & (second_local >= 0) & (second_local < nu_dev)
    )
    local_row = jnp.where(owned, first_local * nu_dev + second_local, 0)
    flat_prev = previous.reshape(mu_dev * nu_dev, prev_count)
    picked = jnp.where(
        owned[:, None], flat_prev.at[local_row].get(mode="promise_in_bounds"), jnp.zeros((), BF16)
    )
    parts, new_vectors = fused(
        picked.reshape(R, count // R, prev_count), pivot_columns, previous, pivot_inverse, orbitals, R, G
    )
    parts = parts.reshape(G, R * mu_dev * (count // R), orbitals.shape[1] // G)
    return new_vectors, orbital_block(parts, slab_orbitals)


def solution(mesh):
    R, G = mesh.shape["rows"], mesh.shape["grp"]
    in_specs = (P("rows", "grp", None), P("rows", "grp", None), P(), P(), P("grp", None), P())
    out_specs = (P("rows", "grp", None), P("rows", None, "grp"))
    return jax.shard_map(
        functools.partial(per_device, R, G), mesh=mesh, in_specs=in_specs, out_specs=out_specs,
        check_vma=False,
    )
```

profile of v0, /device:TPU:0, one launch (start us, length us, event | category | flops | bytes accessed | tf_op | source)
XLA Modules:
  0.0 91.6 jit_solution(9356280429620039551)
XLA Ops:
  0.6 0.7 compare_select_fusion
  1.3 0.1 broadcast_in_dim.20
  1.4 6.5 %gather_fusion = bf16[256,512]{1,0:T(8,128)(2,1)S(1)} fusion(bf16[10240,512]{1,0:T(8,128)(2,1)} %bitcast.3, s32[1024]{0:T(1024)S(1)} %pad_clamp_fusion), kind=kCustom, calls=%fused_computation | custom fusion | bytes 525312 | tf_op jit(solution)/shard_map/gather | solution.py:315
  8.0 0.8 broadcast_select_fusion.x_ref
  8.8 64.9 %fused_exchange.1 = (bf16[128,32,256]{2,1,0:T(8,128)(2,1)}, bf16[4,2560,256]{2,1,0:T(8,128)(2,1)}) custom-call(bf16[8,32,512]{2,1,0:T(8,128)(2,1)} %broadcast_select_fusion.x_ref, bf16[4,2560,256]{2,1,0:T(8,128)(2,1)} %pc_hbm.1, bf16[4,2560,512]{2,1,0:T(8,128)(2,1)} %prev_hbm.1, bf16[256,256]{1,0:T(8,128)(2,1)} %inv_ref.1, bf16[2560,1024]{1,0:T(8,128)(2,1)} %orb_hbm.1), custom_call_target="tpu_custom_call" | custom-call | tf_op jit(solution)/shard_map/fused_exchange/pallas_call | solution.py:205
  73.7 12.8 %orbital_block.1 = bf16[32,1024,256]{2,1,0:T(8,128)(2,1)} custom-call(bf16[4,1024,256]{2,1,0:T(8,128)(2,1)} %bitcast.4, bf16[32,1024]{1,0:T(8,128)(2,1)} %slab_ref.1), custom_call_target="tpu_custom_call" | custom-call | tf_op jit(solution)/shard_map/orbital_block/pallas_call | solution.py:283
  86.5 5.2 %copy.9 = bf16[4,2560,256]{2,1,0:T(8,128)(2,1)} copy(bf16[4,2560,256]{2,1,0:T(8,128)(2,1)} %get-tuple-element.10) | data formatting | bytes 10485760
  (1 shorter events, 0.0 us)
where the time goes:
time: 91.9 us; the launch traced here: 91.6 us
  Pallas kernels  77.7 us (85%)
  local copies, waits for them, and re-layouts  11.8 us (13%)
  other arithmetic  1.51 us (2%)
    pallas_call x1, Pallas kernels, fused(): pl.pallas_call(functools.partial(fused_kernel, R, G), out_shape=(jax.Shap...  64.9 us
    pallas_call x1, Pallas kernels, orbital_block(): pl.pallas_call(block_kernel, grid=(vecs // block,), out_shape=jax.ShapeDt...  12.8 us
    gather x1, local copies, waits for them, and re-layouts, per_device(): flat_prev.at[local_row].get(mode='promise_in_bounds')  6.54 us
    unnamed x1, local copies, waits for them, and re-layouts  5.18 us

commit v1 on v0

v1 whole, which is shorter than its diff:
```python
import functools

import jax
import jax.numpy as jnp
from jax import lax
from jax.experimental import pallas as pl
from jax.experimental.pallas import tpu as pltpu
from jax.sharding import PartitionSpec as P

F32 = jnp.float32
BF16 = jnp.bfloat16
MESH = pl.DeviceIdType.MESH


def chained(G):
    return G <= 4


def group_orders(G):
    def due(g, d):
        if d == g:
            return 4 * G
        return 2 * (G - 1 - d) + g if d > g else 2 * d + G - 1 - g

    return [sorted(range(G), key=lambda d: (due(g, d), d)) for g in range(G)]


def choose(g, values):
    chosen = jnp.int32(values[0])
    for k in range(1, len(values)):
        chosen = jnp.where(g == k, values[k], chosen)
    return chosen


def fused_kernel(
    R, G, piv_ref, pc_hbm, prev_hbm, inv_ref, orb_hbm, out_hbm, new_v,
    piv_col, picked, buf_x, buf_a, buf_b, buf_c, rows_v, upper_v, prev_v, orb_v, turned, block_v, send, in_up, in_down,
    send_a, recv_a, send_b, recv_b, send_c, recv_c, prev_sem, pc_sem, orb_sem,
    own_sem, hop_sem, up_sem, down_sem, send_sem, recv_sem,
):
    r = lax.axis_index("rows")
    g = lax.axis_index("grp")
    N = R * G
    me = r * G + g
    mu_dev, nu, p = new_v.shape
    _, _, _, pl_dev, j_dev = send.shape
    c = buf_c.shape[1]

    load_prev = [pltpu.make_async_copy(prev_hbm.at[mu], prev_v.at[mu], prev_sem.at[mu]) for mu in range(mu_dev)]
    load_orb = pltpu.make_async_copy(orb_hbm, orb_v, orb_sem)

    def load_pc(mu):
        return pltpu.make_async_copy(pc_hbm.at[mu], new_v.at[mu], pc_sem.at[mu])

    for copy in load_prev:
        copy.start()
    for mu in range(mu_dev):
        load_pc(mu).start()
    load_orb.start()

    barrier = pltpu.get_barrier_semaphore()

    @pl.loop(1, N)
    def _(d):
        peer = lax.rem(me + d, N)
        pl.semaphore_signal(
            barrier, inc=1, device_id={"rows": peer // G, "grp": lax.rem(peer, G)}, device_id_type=MESH
        )

    shape = (p, p)
    low = lax.broadcasted_iota(jnp.int32, shape, 0)
    high = lax.broadcasted_iota(jnp.int32, shape, 1)
    upper_v[...] = jnp.where(low <= high, inv_ref[...].astype(F32), 0.0).astype(BF16)

    lanes = piv_col.shape[1]
    piv_col[...] = jnp.broadcast_to(piv_ref[...], (lanes, p)).T
    picked[...] = jnp.zeros(picked.shape, F32)
    piece = 512 if nu % 512 == 0 else 256
    for mu in range(mu_dev):
        load_prev[mu].wait()
        base = (r * mu_dev + mu) * (nu * G) + g * nu

        @pl.loop(0, nu // piece)
        def _(i):
            start = pl.multiple_of(i * piece, piece)
            at = lax.broadcasted_iota(jnp.int32, (p, lanes), 1) + (base + start)
            hot = jnp.concatenate(
                [jnp.where(piv_col[...] == at + k * lanes, 1.0, 0.0).astype(BF16) for k in range(piece // lanes)], axis=1
            )
            picked[...] += jnp.dot(hot, prev_v[mu, pl.ds(start, piece), :], preferred_element_type=F32)

    for k in range(R):
        buf_x[k] = picked[k * c : (k + 1) * c, :].astype(BF16)
    pl.semaphore_wait(barrier, N - 1)

    def remote(src, dst, send, recv, row, grp):
        return pltpu.make_async_remote_copy(
            src_ref=src, dst_ref=dst, send_sem=send, recv_sem=recv,
            device_id={"rows": row, "grp": grp}, device_id_type=MESH,
        )

    row_peers = [(d, lax.rem(r + d, R)) for d in range(1, R)]
    grp_peers = [(d, lax.rem(g + d, G)) for d in range(1, G)]
    first = [remote(buf_x.at[q], buf_a.at[d], send_a.at[d], recv_a.at[d], q, g) for d, q in row_peers]
    for copy in first:
        copy.start()
    total = buf_x[r].astype(F32)
    for (d, _), copy in zip(row_peers, first):
        copy.wait_recv()
        total = total + buf_a[d].astype(F32)
    buf_b[0] = total.astype(BF16)
    second = [remote(buf_b.at[0], buf_b.at[d], send_b.at[d], recv_b.at[d], r, q) for d, q in grp_peers]
    for copy in second:
        copy.start()
    for (d, _), copy in zip(grp_peers, second):
        copy.wait_recv()
        total = total + buf_b[d].astype(F32)
    buf_c[r] = total.astype(BF16)
    third = [remote(buf_c.at[r], buf_c.at[r], send_c.at[d], recv_c.at[d], q, g) for d, q in row_peers]
    for copy in third:
        copy.start()
    for copy in third:
        copy.wait_recv()
    for copy in first + second + third:
        copy.wait_send()
    for k in range(R):
        picked[k * c : (k + 1) * c, :] = buf_c[k].astype(F32)
    rows_v[...] = picked[...].astype(BF16)
    load_orb.wait()

    chunk = 512 if nu % 512 == 0 else 256
    orders = group_orders(G)

    def make_vectors(mu):
        load_pc(mu).wait()
        eye = jnp.where(
            lax.broadcasted_iota(jnp.int32, shape, 0) == lax.broadcasted_iota(jnp.int32, shape, 1), 1.0, 0.0
        ).astype(BF16)

        @pl.loop(0, nu // chunk)
        def _(i):
            at = pl.ds(pl.multiple_of(i * chunk, chunk), chunk)
            correction = lax.dot_general(
                prev_v[mu, at, :], rows_v[...], (((1,), (1,)), ((), ())), preferred_element_type=F32
            )
            residual = (new_v[mu, at, :].astype(F32) - correction).astype(BF16)
            made = jnp.dot(residual, upper_v[...], preferred_element_type=F32).astype(BF16)
            new_v[mu, at, :] = made
            turned[mu, :, at] = lax.dot_general(
                eye, made, (((1,), (1,)), ((), ())), preferred_element_type=F32
            ).astype(BF16)

    def add(buf, slot, sem, mu):
        here = buf.at[slot, mu]
        pltpu.make_async_copy(here, here, sem.at[slot, mu]).wait()
        for k in range(R):
            block_v[k * pl_dev : (k + 1) * pl_dev, :] += buf[slot, mu, k].astype(F32)

    for s in range(G):
        to = choose(g, [order[s] for order in orders])
        own = s == G - 1

        @pl.loop(0, mu_dev)
        def _(mu):
            if s == 0:
                make_vectors(mu)
            cols = pl.ds(pl.multiple_of(to * j_dev, j_dev), j_dev)
            block_v[...] = jnp.dot(turned[mu], orb_v[:, cols], preferred_element_type=F32)
            if chained(G):
                if G > 1:
                    pl.when((to >= g) & (g > 0))(lambda: add(in_up, to, up_sem, mu))
                    pl.when((to <= g) & (g < G - 1))(lambda: add(in_down, to, down_sem, mu))
            elif own:
                for d, q in grp_peers:
                    add(in_up, q, up_sem, mu)
            for k in range(R):
                send[to, mu, k] = block_v[k * pl_dev : (k + 1) * pl_dev, :].astype(BF16)
            if own:
                for k in range(R):
                    peer = lax.rem(r + k, R)
                    src = send.at[to, mu, peer]
                    dst = out_hbm.at[r * mu_dev + mu]
                    if k:
                        remote(src, dst, send_sem, recv_sem, peer, g).start()
                    else:
                        pltpu.make_async_copy(src, dst, own_sem).start()
            elif chained(G):
                @pl.when(to > g)
                def _():
                    remote(send.at[to, mu], in_up.at[to, mu], hop_sem, up_sem.at[to, mu], r, g + 1).start()

                @pl.when(to < g)
                def _():
                    remote(send.at[to, mu], in_down.at[to, mu], hop_sem, down_sem.at[to, mu], r, g - 1).start()
            else:
                remote(send.at[to, mu], in_up.at[g, mu], hop_sem, up_sem.at[g, mu], r, to).start()

    own = out_hbm.at[pl.ds(0, mu_dev)]
    pltpu.make_async_copy(own, own, own_sem).wait()
    if G > 1:
        hops = send.at[pl.ds(0, G - 1)]
        pltpu.make_async_copy(hops, hops, hop_sem).wait()
    if R > 1:
        every = out_hbm.at[pl.ds(0, (R - 1) * mu_dev)]
        pltpu.make_async_copy(every, every, send_sem).wait()
        pltpu.make_async_copy(every, every, recv_sem).wait()


def fused(pivots, columns, previous, inverse, orbitals, R, G):
    mu_dev, nu, p = columns.shape
    k = previous.shape[2]
    c = p // R
    nj = orbitals.shape[1]
    hbm = pl.BlockSpec(memory_space=pl.ANY)
    vmem = pl.BlockSpec(memory_space=pltpu.VMEM)
    dma = pltpu.SemaphoreType.DMA
    return pl.pallas_call(
        functools.partial(fused_kernel, R, G),
        out_shape=(
            jax.ShapeDtypeStruct((R * mu_dev, c, nj // G), BF16),
            jax.ShapeDtypeStruct(columns.shape, BF16),
        ),
        in_specs=[vmem, hbm, hbm, vmem, hbm],
        out_specs=(hbm, vmem),
        scratch_shapes=[
            pltpu.VMEM((p, 128), jnp.int32),
            pltpu.VMEM((p, k), F32),
            pltpu.VMEM((R, c, k), BF16),
            pltpu.VMEM((R, c, k), BF16),
            pltpu.VMEM((G, c, k), BF16),
            pltpu.VMEM((R, c, k), BF16),
            pltpu.VMEM((p, k), BF16),
            pltpu.VMEM((p, p), BF16),
            pltpu.VMEM((mu_dev, nu, k), BF16),
            pltpu.VMEM((nu, nj), BF16),
            pltpu.VMEM((mu_dev, p, nu), BF16),
            pltpu.VMEM((p, nj // G), F32),
            pltpu.VMEM((G, mu_dev, R, c, nj // G), BF16),
            pltpu.VMEM((G, mu_dev, R, c, nj // G), BF16),
            pltpu.VMEM((G, mu_dev, R, c, nj // G), BF16),
            dma((R,)), dma((R,)), dma((G,)), dma((G,)), dma((R,)), dma((R,)),
            dma((mu_dev,)), dma((mu_dev,)), dma(()),
            dma(()), dma(()), dma((G, mu_dev)), dma((G, mu_dev)), dma(()), dma(()),
        ],
        compiler_params=pltpu.CompilerParams(
            collective_id=0, has_side_effects=True, vmem_limit_bytes=48 * 1024 * 1024
        ),
        name="fused_exchange",
    )(pivots, columns, previous, inverse, orbitals)


def block_kernel(part_ref, slab_ref, made_ref, out_ref, new_hbm, sorted_ref, slab_t_ref, new_sem):
    rows, _ = part_ref.shape
    mus = slab_ref.shape[0]
    block = out_ref.shape[0]
    vecs = rows // mus
    step = pl.program_id(0)
    store = pltpu.make_async_copy(made_ref, new_hbm, new_sem)

    @pl.when(step == 0)
    def _():
        store.start()
        slab_t_ref[...] = slab_ref[...].astype(F32).T.astype(BF16)
        piece = 128
        shift = mus.bit_length() - 1

        @pl.loop(0, rows // piece)
        def _(i):
            at = pl.ds(pl.multiple_of(i * piece, piece), piece)
            row = lax.broadcasted_iota(jnp.int32, (piece, rows), 0) + i * piece
            col = lax.broadcasted_iota(jnp.int32, (piece, rows), 1)
            source = (row & (mus - 1)) * vecs + lax.shift_right_logical(row, shift)
            pick = jnp.where(source == col, 1.0, 0.0).astype(BF16)
            sorted_ref[at, :] = jnp.dot(pick, part_ref[...], preferred_element_type=F32).astype(BF16)

    for q in range(block):
        at = pl.ds(pl.multiple_of((step * block + q) * mus, mus), mus)
        out_ref[q] = jnp.dot(slab_t_ref[...], sorted_ref[at, :], preferred_element_type=F32).astype(BF16)

    @pl.when(step == pl.num_programs(0) - 1)
    def _():
        store.wait()


def orbital_block(part, slab, made):
    rows, j = part.shape
    mus, i = slab.shape
    assert mus & (mus - 1) == 0
    vecs = rows // mus
    block = 4 if vecs % 4 == 0 else 1
    return pl.pallas_call(
        block_kernel,
        grid=(vecs // block,),
        out_shape=(
            jax.ShapeDtypeStruct((vecs, i, j), BF16),
            jax.ShapeDtypeStruct(made.shape, BF16),
        ),
        in_specs=[
            pl.BlockSpec((rows, j), lambda s: (0, 0)),
            pl.BlockSpec((mus, i), lambda s: (0, 0)),
            pl.BlockSpec(memory_space=pltpu.VMEM),
        ],
        out_specs=(pl.BlockSpec((block, i, j), lambda s: (s, 0, 0)), pl.BlockSpec(memory_space=pl.ANY)),
        scratch_shapes=[
            pltpu.VMEM((rows, j), BF16),
            pltpu.VMEM((i, mus), BF16),
            pltpu.SemaphoreType.DMA(()),
        ],
        compiler_params=pltpu.CompilerParams(vmem_limit_bytes=40 * 1024 * 1024),
        name="orbital_block",
    )(part, slab, made)


def per_device(R, G, pivot_columns, previous, pivots, pivot_inverse, orbitals, slab_orbitals):
    mu_dev = previous.shape[0]
    count = pivot_columns.shape[2]
    part, made = fused(
        pivots.reshape(1, count), pivot_columns, previous, pivot_inverse, orbitals, R, G
    )
    part = part.reshape(R * mu_dev * (count // R), orbitals.shape[1] // G)
    mo_block, new_vectors = orbital_block(part, slab_orbitals, made)
    return new_vectors, mo_block


def solution(mesh):
    R, G = mesh.shape["rows"], mesh.shape["grp"]
    in_specs = (P("rows", "grp", None), P("rows", "grp", None), P(), P(), P("grp", None), P())
    out_specs = (P("rows", "grp", None), P("rows", None, "grp"))
    return jax.shard_map(
        functools.partial(per_device, R, G), mesh=mesh, in_specs=in_specs, out_specs=out_specs,
        check_vma=False,
    )
```

time: 91.9 us -> 84.7 us (0.922)
  the two profiles are of different devices: /device:TPU:0 before, /device:TPU:9 now
where the time goes in v1:
time: 84.7 us; the launch traced here: 84.5 us
  Pallas kernels  82.3 us (97%)
  local copies, waits for them, and re-layouts  1.58 us (2%)
    pallas_call x1, Pallas kernels, fused(): pl.pallas_call(functools.partial(fused_kernel, R, G), out_shape=(jax.Shap...  71.5 us
    pallas_call x1, Pallas kernels, orbital_block(): pl.pallas_call(block_kernel, grid=(vecs // block,), out_shape=(jax.ShapeD...  10.8 us

profile of v1, /device:TPU:9, one launch (start us, length us, event | category | flops | bytes accessed | tf_op | source)
XLA Modules:
  0.0 84.5 jit_solution(190042336802725632)
XLA Ops:
  0.6 0.0 copy-start
  0.6 0.9 %copy-done = bf16[256,256]{1,0:T(8,128)(2,1)S(1)} copy-done((bf16[256,256]{1,0:T(8,128)(2,1)S(1)}, bf16[256,256]{1,0:T(8,128)(2,1)}, u32[]{:S(2)}) %copy-start) | copy-done | bytes 131096
  1.5 0.0 copy-start.2
  1.5 0.7 copy-done.2
  2.2 0.0 copy-start.1
  2.2 71.5 %fused_exchange.1 = (bf16[32,32,256]{2,1,0:T(8,128)(2,1)S(1)}, bf16[4,2560,256]{2,1,0:T(8,128)(2,1)S(1)}) custom-call(s32[1,256]{1,0:T(1,128)S(1)} %bitcast.3, bf16[4,2560,256]{2,1,0:T(8,128)(2,1)} %pc_hbm.1, bf16[4,2560,512]{2,1,0:T(8,128)(2,1)} %prev_hbm.1, bf16[256,256]{1,0:T(8,128)(2,1)S(1)} %copy-done, bf16[2560,1024]{1,0:T(8,128)(2,1)} %orb_hbm.1), custom_call_target="tpu_custom_call" | custom-call | tf_op jit(solution)/shard_map/fused_exchange/pallas_call | solution.py:217
  73.7 0.0 copy-done.1
  73.7 10.8 %orbital_block.1 = (bf16[32,1024,256]{2,1,0:T(8,128)(2,1)}, bf16[4,2560,256]{2,1,0:T(8,128)(2,1)}) custom-call(bf16[1024,256]{1,0:T(8,128)(2,1)S(1)} %bitcast.2, bf16[32,1024]{1,0:T(8,128)(2,1)S(1)} %copy-done.1, bf16[4,2560,256]{2,1,0:T(8,128)(2,1)S(1)} %get-tuple-element.7.made_ref), custom_call_target="tpu_custom_call" | custom-call | tf_op jit(solution)/shard_map/orbital_block/pallas_call | solution.py:291
Async XLA Ops:
  0.6 0.9 %copy-start = (bf16[256,256]{1,0:T(8,128)(2,1)S(1)}, bf16[256,256]{1,0:T(8,128)(2,1)}, u32[]{:S(2)}) copy-start(bf16[256,256]{1,0:T(8,128)(2,1)} %inv_ref.1) | copy-start | bytes 393220
  1.5 0.7 copy-start.2
  2.2 71.5 %copy-start.1 = (bf16[32,1024]{1,0:T(8,128)(2,1)S(1)}, bf16[32,1024]{1,0:T(8,128)(2,1)}, u32[]{:S(2)}) copy-start(bf16[32,1024]{1,0:T(8,128)(2,1)} %slab_ref.1) | copy-start | bytes 196612

commit v2 on v1

v2 whole, which is shorter than its diff:
```python
import functools

import jax
import jax.numpy as jnp
from jax import lax
from jax.experimental import pallas as pl
from jax.experimental.pallas import tpu as pltpu
from jax.sharding import PartitionSpec as P

F32 = jnp.float32
BF16 = jnp.bfloat16
MESH = pl.DeviceIdType.MESH


def chained(G):
    return G <= 4


def group_orders(G):
    def due(g, d):
        if d == g:
            return 4 * G
        return 2 * (G - 1 - d) + g if d > g else 2 * d + G - 1 - g

    return [sorted(range(G), key=lambda d: (due(g, d), d)) for g in range(G)]


def choose(g, values):
    chosen = jnp.int32(values[0])
    for k in range(1, len(values)):
        chosen = jnp.where(g == k, values[k], chosen)
    return chosen


def fused_kernel(
    R, G, piv_hbm, pc_hbm, prev_hbm, inv_hbm, orb_hbm, out_hbm, new_v,
    piv_v, inv_v, piv_col, hot_v, picked, buf_x, buf_a, buf_b, buf_c, rows_t, upper_v, prev_v, orb_v, orb_t,
    block_v, send, in_up, in_down, fin_v,
    send_a, recv_a, send_b, recv_b, send_c, recv_c, small_sem, prev_sem, pc_sem, orb_sem,
    own_sem, hop_sem, up_sem, down_sem, send_sem, recv_sem,
):
    r = lax.axis_index("rows")
    g = lax.axis_index("grp")
    N = R * G
    me = r * G + g
    mu_dev, nu, p = new_v.shape
    _, _, j_dev, _ = send.shape
    halves, _, c, kh = buf_c.shape

    load_piv = pltpu.make_async_copy(piv_hbm, piv_v, small_sem.at[0])
    load_inv = pltpu.make_async_copy(inv_hbm, inv_v, small_sem.at[1])
    load_orb = pltpu.make_async_copy(orb_hbm, orb_v, orb_sem)

    def load_prev(h, mu):
        at = pl.ds(h * kh, kh)
        return pltpu.make_async_copy(prev_hbm.at[mu, :, at], prev_v.at[mu, :, at], prev_sem.at[h, mu])

    def load_pc(mu):
        return pltpu.make_async_copy(pc_hbm.at[mu], new_v.at[mu], pc_sem.at[mu])

    load_piv.start()
    for h in range(halves):
        for mu in range(mu_dev):
            load_prev(h, mu).start()
    load_inv.start()

    barrier = pltpu.get_barrier_semaphore()

    @pl.loop(1, N)
    def _(d):
        peer = lax.rem(me + d, N)
        pl.semaphore_signal(
            barrier, inc=1, device_id={"rows": peer // G, "grp": lax.rem(peer, G)}, device_id_type=MESH
        )

    lanes = piv_col.shape[1]
    load_piv.wait()
    piv_col[...] = jnp.broadcast_to(piv_v[...], (lanes, p)).T
    for mu in range(mu_dev):
        base = (r * mu_dev + mu) * (nu * G) + g * nu

        @pl.loop(0, nu // lanes)
        def _(i):
            start = pl.multiple_of(i * lanes, lanes)
            at = lax.broadcasted_iota(jnp.int32, (p, lanes), 1) + (base + start)
            hot_v[mu, :, pl.ds(start, lanes)] = jnp.where(piv_col[...] == at, 1.0, 0.0).astype(BF16)

    def remote(src, dst, send, recv, row, grp):
        return pltpu.make_async_remote_copy(
            src_ref=src, dst_ref=dst, send_sem=send, recv_sem=recv,
            device_id={"rows": row, "grp": grp}, device_id_type=MESH,
        )

    row_peers = [(d, lax.rem(r + d, R)) for d in range(1, R)]
    grp_peers = [(d, lax.rem(g + d, G)) for d in range(1, G)]

    def pick(h):
        picked[...] = jnp.zeros(picked.shape, F32)

        @pl.loop(0, mu_dev)
        def _(mu):
            load_prev(h, mu).wait()
            picked[...] += jnp.dot(hot_v[mu], prev_v[mu, :, h * kh : (h + 1) * kh], preferred_element_type=F32)

        for k in range(R):
            buf_x[h, k] = picked[k * c : (k + 1) * c, :].astype(BF16)

    def first(h):
        return [
            remote(buf_x.at[h, q], buf_a.at[h, d], send_a.at[h, d], recv_a.at[h, d], q, g) for d, q in row_peers
        ]

    def second(h):
        return [
            remote(buf_b.at[h, 0], buf_b.at[h, d], send_b.at[h, d], recv_b.at[h, d], r, q) for d, q in grp_peers
        ]

    def third(h):
        return [
            remote(buf_c.at[h, r], buf_c.at[h, r], send_c.at[h, d], recv_c.at[h, d], q, g) for d, q in row_peers
        ]

    def add_rows(h):
        total = buf_x[h, r].astype(F32)
        for (d, _), copy in zip(row_peers, first(h)):
            copy.wait_recv()
            total = total + buf_a[h, d].astype(F32)
        buf_b[h, 0] = total.astype(BF16)
        for copy in second(h):
            copy.start()

    def add_groups(h):
        total = buf_b[h, 0].astype(F32)
        for (d, _), copy in zip(grp_peers, second(h)):
            copy.wait_recv()
            total = total + buf_b[h, d].astype(F32)
        buf_c[h, r] = total.astype(BF16)
        for copy in third(h):
            copy.start()

    def take_rows(h):
        for copy in third(h):
            copy.wait_recv()
        for k in range(R):
            picked[k * c : (k + 1) * c, :] = buf_c[h, k].astype(F32)
        rows_t[h * kh : (h + 1) * kh, :] = picked[...].T.astype(BF16)

    square = (256, 256)
    eye = jnp.where(
        lax.broadcasted_iota(jnp.int32, square, 0) == lax.broadcasted_iota(jnp.int32, square, 1), 1.0, 0.0
    ).astype(BF16)
    wide = orb_v.shape[1] // 256

    def turn_orbitals(first, last):
        @pl.loop(first, last)
        def _(i):
            at = pl.ds(pl.multiple_of(i * 256, 256), 256)
            for q in range(wide):
                orb_t[q * 256 : (q + 1) * 256, at] = lax.dot_general(
                    eye, orb_v[at, q * 256 : (q + 1) * 256], (((1,), (1,)), ((), ())), preferred_element_type=F32
                ).astype(BF16)

    tiles = nu // 256
    cuts = [tiles * k // (2 * halves) for k in range(2 * halves + 1)]
    for h in range(halves):
        pick(h)
        if h == 0:
            load_orb.start()
            for mu in range(mu_dev):
                load_pc(mu).start()
            pl.semaphore_wait(barrier, N - 1)
        for copy in first(h):
            copy.start()
    load_inv.wait()
    low = lax.broadcasted_iota(jnp.int32, (p, p), 0)
    high = lax.broadcasted_iota(jnp.int32, (p, p), 1)
    upper_v[...] = jnp.where(low <= high, inv_v[...].astype(F32), 0.0).astype(BF16)
    load_orb.wait()
    for h in range(halves):
        add_rows(h)
        turn_orbitals(cuts[h], cuts[h + 1])
    for h in range(halves):
        add_groups(h)
        turn_orbitals(cuts[halves + h], cuts[halves + h + 1])
    for h in range(halves):
        take_rows(h)

    chunk = 512 if nu % 512 == 0 else 256
    orders = group_orders(G)

    def make_vectors(mu):
        load_pc(mu).wait()
        for i in range(nu // chunk):
            at = pl.ds(i * chunk, chunk)
            correction = jnp.dot(prev_v[mu, at, :], rows_t[...], preferred_element_type=F32)
            residual = (new_v[mu, at, :].astype(F32) - correction).astype(BF16)
            new_v[mu, at, :] = jnp.dot(residual, upper_v[...], preferred_element_type=F32).astype(BF16)

    def add(buf, slot, sem, mu):
        here = buf.at[slot, mu]
        pltpu.make_async_copy(here, here, sem.at[slot, mu]).wait()
        block_v[...] += buf[slot, mu].astype(F32)

    for s in range(G):
        to = choose(g, [order[s] for order in orders])
        own = s == G - 1

        @pl.loop(0, mu_dev)
        def _(mu):
            if s == 0:
                make_vectors(mu)
            at = pl.ds(pl.multiple_of(to * j_dev, j_dev), j_dev)
            block_v[...] = jnp.dot(orb_t[at, :], new_v[mu], preferred_element_type=F32)
            if chained(G):
                if G > 1:
                    pl.when((to >= g) & (g > 0))(lambda: add(in_up, to, up_sem, mu))
                    pl.when((to <= g) & (g < G - 1))(lambda: add(in_down, to, down_sem, mu))
            elif own:
                for d, q in grp_peers:
                    add(in_up, q, up_sem, mu)
            if own:
                half = block_v[...].T.astype(BF16)
                for k in range(R):
                    fin_v[mu, k] = half[k * c : (k + 1) * c, :]
                for k in range(R):
                    peer = lax.rem(r + k, R)
                    src = fin_v.at[mu, peer]
                    dst = out_hbm.at[r * mu_dev + mu]
                    if k:
                        remote(src, dst, send_sem, recv_sem, peer, g).start()
                    else:
                        pltpu.make_async_copy(src, dst, own_sem).start()
                return
            send[to, mu] = block_v[...].astype(BF16)
            if chained(G):
                @pl.when(to > g)
                def _():
                    remote(send.at[to, mu], in_up.at[to, mu], hop_sem, up_sem.at[to, mu], r, g + 1).start()

                @pl.when(to < g)
                def _():
                    remote(send.at[to, mu], in_down.at[to, mu], hop_sem, down_sem.at[to, mu], r, g - 1).start()
            else:
                remote(send.at[to, mu], in_up.at[g, mu], hop_sem, up_sem.at[g, mu], r, to).start()

    for h in range(halves):
        for copy in first(h) + second(h) + third(h):
            copy.wait_send()
    own = out_hbm.at[pl.ds(0, mu_dev)]
    pltpu.make_async_copy(own, own, own_sem).wait()
    if G > 1:
        hops = send.at[pl.ds(0, G - 1)]
        pltpu.make_async_copy(hops, hops, hop_sem).wait()
    if R > 1:
        every = out_hbm.at[pl.ds(0, (R - 1) * mu_dev)]
        pltpu.make_async_copy(every, every, send_sem).wait()
        pltpu.make_async_copy(every, every, recv_sem).wait()


def fused(pivots, columns, previous, inverse, orbitals, R, G):
    mu_dev, nu, p = columns.shape
    k = previous.shape[2]
    c = p // R
    nj = orbitals.shape[1]
    halves = 2
    kh = k // halves
    hbm = pl.BlockSpec(memory_space=pltpu.HBM)
    anywhere = pl.BlockSpec(memory_space=pl.ANY)
    vmem = pl.BlockSpec(memory_space=pltpu.VMEM)
    dma = pltpu.SemaphoreType.DMA
    return pl.pallas_call(
        functools.partial(fused_kernel, R, G),
        out_shape=(
            jax.ShapeDtypeStruct((R * mu_dev, c, nj // G), BF16),
            jax.ShapeDtypeStruct(columns.shape, BF16),
        ),
        in_specs=[hbm, hbm, hbm, hbm, hbm],
        out_specs=(anywhere, vmem),
        scratch_shapes=[
            pltpu.VMEM((1, p), jnp.int32),
            pltpu.VMEM((p, p), BF16),
            pltpu.VMEM((p, 128), jnp.int32),
            pltpu.VMEM((mu_dev, p, nu), BF16),
            pltpu.VMEM((p, kh), F32),
            pltpu.VMEM((halves, R, c, kh), BF16),
            pltpu.VMEM((halves, R, c, kh), BF16),
            pltpu.VMEM((halves, G, c, kh), BF16),
            pltpu.VMEM((halves, R, c, kh), BF16),
            pltpu.VMEM((k, p), BF16),
            pltpu.VMEM((p, p), BF16),
            pltpu.VMEM((mu_dev, nu, k), BF16),
            pltpu.VMEM((nu, nj), BF16),
            pltpu.VMEM((nj, nu), BF16),
            pltpu.VMEM((nj // G, p), F32),
            pltpu.VMEM((G, mu_dev, nj // G, p), BF16),
            pltpu.VMEM((G, mu_dev, nj // G, p), BF16),
            pltpu.VMEM((G, mu_dev, nj // G, p), BF16),
            pltpu.VMEM((mu_dev, R, c, nj // G), BF16),
            dma((halves, R)), dma((halves, R)), dma((halves, G)), dma((halves, G)), dma((halves, R)), dma((halves, R)),
            dma((2,)), dma((halves, mu_dev)), dma((mu_dev,)), dma(()),
            dma(()), dma(()), dma((G, mu_dev)), dma((G, mu_dev)), dma(()), dma(()),
        ],
        compiler_params=pltpu.CompilerParams(
            collective_id=0, has_side_effects=True, vmem_limit_bytes=44 * 1024 * 1024
        ),
        name="fused_exchange",
    )(pivots, columns, previous, inverse, orbitals)


def block_kernel(part_ref, slab_ref, made_ref, out_ref, new_hbm, part_v, spread_ref, new_sem):
    mus, vecs, _ = part_ref.shape
    groups, _, _, j = out_ref.shape
    lot = vecs // groups
    wide = mus * lot
    step = pl.program_id(0)
    store = pltpu.make_async_copy(made_ref, new_hbm, new_sem)

    @pl.when(step == 0)
    def _():
        store.start()
        mu = lax.broadcasted_iota(jnp.int32, (mus, wide), 0)
        col = lax.broadcasted_iota(jnp.int32, (mus, wide), 1)
        repeat = jnp.where(lax.shift_right_logical(col, lot.bit_length() - 1) == mu, 1.0, 0.0).astype(BF16)
        spread_ref[...] = lax.dot_general(
            slab_ref[...], repeat, (((0,), (0,)), ((), ())), preferred_element_type=F32
        ).astype(BF16)
        for k in range(groups):
            part_v[:, k * j : (k + 1) * j] = part_ref[:, k * lot : (k + 1) * lot, :].reshape(wide, j)

    col = lax.broadcasted_iota(jnp.int32, spread_ref.shape, 1) & (lot - 1)
    kept = jnp.where(col == step, spread_ref[...].astype(F32), 0.0).astype(BF16)
    for k in range(groups):
        out_ref[k, 0] = jnp.dot(kept, part_v[:, k * j : (k + 1) * j], preferred_element_type=F32).astype(BF16)

    @pl.when(step == pl.num_programs(0) - 1)
    def _():
        store.wait()


def orbital_block(part, slab, made):
    mus, vecs, j = part.shape
    i = slab.shape[1]
    lot = 8
    assert vecs % lot == 0
    out, new = pl.pallas_call(
        block_kernel,
        grid=(lot,),
        out_shape=(
            jax.ShapeDtypeStruct((vecs // lot, lot, i, j), BF16),
            jax.ShapeDtypeStruct(made.shape, BF16),
        ),
        in_specs=[
            pl.BlockSpec(memory_space=pltpu.VMEM),
            pl.BlockSpec((mus, i), lambda s: (0, 0)),
            pl.BlockSpec(memory_space=pltpu.VMEM),
        ],
        out_specs=(
            pl.BlockSpec((vecs // lot, 1, i, j), lambda s: (0, s, 0, 0)), pl.BlockSpec(memory_space=pl.ANY)
        ),
        scratch_shapes=[
            pltpu.VMEM((mus * lot, vecs // lot * j), BF16),
            pltpu.VMEM((i, mus * lot), BF16),
            pltpu.SemaphoreType.DMA(()),
        ],
        compiler_params=pltpu.CompilerParams(vmem_limit_bytes=40 * 1024 * 1024),
        name="orbital_block",
    )(part, slab, made)
    return out.reshape(vecs, i, j), new


def per_device(R, G, pivot_columns, previous, pivots, pivot_inverse, orbitals, slab_orbitals):
    count = pivot_columns.shape[2]
    stay = functools.partial(pltpu.with_memory_space_constraint, memory_space=pltpu.HBM)
    part, made = fused(
        stay(pivots.reshape(1, count)), pivot_columns, previous, stay(pivot_inverse), orbitals, R, G
    )
    mo_block, new_vectors = orbital_block(part, slab_orbitals, made)
    return new_vectors, mo_block


def solution(mesh):
    R, G = mesh.shape["rows"], mesh.shape["grp"]
    in_specs = (P("rows", "grp", None), P("rows", "grp", None), P(), P(), P("grp", None), P())
    out_specs = (P("rows", "grp", None), P("rows", None, "grp"))
    return jax.shard_map(
        functools.partial(per_device, R, G), mesh=mesh, in_specs=in_specs, out_specs=out_specs,
        check_vma=False,
    )
```

time: 84.7 us -> 75.3 us (0.89)
  Pallas kernels: 82.3 us -> 74.5 us
  local copies, waits for them, and re-layouts: 1.58 us -> 0.01 us
    pallas_call x1, Pallas kernels: 71.5 us -> 64.6 us  [fused(): pl.pallas_call(functools.partial(fused_kernel, R, G), out_shape=(jax.Shap...]
    unnamed x6 -> x2, local copies, waits for them, and re-layouts: 1.58 us -> 0.01 us
    pallas_call x1, Pallas kernels: 10.8 us -> 9.89 us  [orbital_block(): pl.pallas_call(block_kernel, grid=(lot,), out_shape=(jax.ShapeDtypeStruct...]
where the time goes in v2:
time: 75.3 us; the launch traced here: 75.2 us
  Pallas kernels  74.5 us (99%)
    pallas_call x1, Pallas kernels, fused(): pl.pallas_call(functools.partial(fused_kernel, R, G), out_shape=(jax.Shap...  64.6 us
    pallas_call x1, Pallas kernels, orbital_block(): pl.pallas_call(block_kernel, grid=(lot,), out_shape=(jax.ShapeDtypeStruct...  9.89 us

profile of v2, /device:TPU:9, one launch (start us, length us, event | category | flops | bytes accessed | tf_op | source)
XLA Modules:
  0.0 75.2 jit_solution(8457120898608936317)
XLA Ops:
  0.6 0.0 copy-start
  0.6 64.6 %fused_exchange.1 = (bf16[32,32,256]{2,1,0:T(8,128)(2,1)S(1)}, bf16[4,2560,256]{2,1,0:T(8,128)(2,1)S(1)}) custom-call(s32[1,256]{1,0:T(1,128)} %bitcast.2, bf16[4,2560,256]{2,1,0:T(8,128)(2,1)} %pc_hbm.1, bf16[4,2560,512]{2,1,0:T(8,128)(2,1)} %prev_hbm.1, bf16[256,256]{1,0:T(8,128)(2,1)} %inv_hbm.1, bf16[2560,1024]{1,0:T(8,128)(2,1)} %orb_hbm.1), custom_call_target="tpu_custom_call" | custom-call | tf_op jit(solution)/shard_map/fused_exchange/pallas_call | solution.py:271
  65.3 0.0 copy-done
  65.3 9.9 %orbital_block.1 = (bf16[4,8,1024,256]{3,2,1,0:T(8,128)(2,1)}, bf16[4,2560,256]{2,1,0:T(8,128)(2,1)}) custom-call(bf16[32,32,256]{2,1,0:T(8,128)(2,1)S(1)} %get-tuple-element.6.part_ref, bf16[32,1024]{1,0:T(8,128)(2,1)S(1)} %copy-done, bf16[4,2560,256]{2,1,0:T(8,128)(2,1)S(1)} %get-tuple-element.7.made_ref), custom_call_target="tpu_custom_call" | custom-call | tf_op jit(solution)/shard_map/orbital_block/pallas_call | solution.py:345
Async XLA Ops:
  0.6 64.7 %copy-start = (bf16[32,1024]{1,0:T(8,128)(2,1)S(1)}, bf16[32,1024]{1,0:T(8,128)(2,1)}, u32[]{:S(2)}) copy-start(bf16[32,1024]{1,0:T(8,128)(2,1)} %slab_ref.1) | copy-start | bytes 196612

commit v3 on v2

--- a/solution.py
+++ b/solution.py
@@ -18,11 +18,11 @@
 
 def group_orders(G):
     def due(g, d):
-        if d == g:
-            return 4 * G
         return 2 * (G - 1 - d) + g if d > g else 2 * d + G - 1 - g
 
-    return [sorted(range(G), key=lambda d: (due(g, d), d)) for g in range(G)]
+    place = max(G - 2, 0)
+    orders = [sorted((d for d in range(G) if d != g), key=lambda d: (due(g, d), d)) for g in range(G)]
+    return [order[:place] + [g] + order[place:] for g, order in enumerate(orders)], place
 
 
 def choose(g, values):
@@ -33,11 +33,11 @@
 
 
 def fused_kernel(
-    R, G, piv_hbm, pc_hbm, prev_hbm, inv_hbm, orb_hbm, out_hbm, new_v,
+    R, G, piv_hbm, pc_hbm, prev_hbm, inv_hbm, orb_hbm, out_v, new_v,
     piv_v, inv_v, piv_col, hot_v, picked, buf_x, buf_a, buf_b, buf_c, rows_t, upper_v, prev_v, orb_v, orb_t,
-    block_v, send, in_up, in_down, fin_v,
+    block_v, send, in_up, in_down, last, own_out, last_in, own_in,
     send_a, recv_a, send_b, recv_b, send_c, recv_c, small_sem, prev_sem, pc_sem, orb_sem,
-    own_sem, hop_sem, up_sem, down_sem, send_sem, recv_sem,
+    hop_sem, up_sem, down_sem, last_send, last_recv, own_send, own_recv,
 ):
     r = lax.axis_index("rows")
     g = lax.axis_index("grp")
@@ -59,11 +59,6 @@
         return pltpu.make_async_copy(pc_hbm.at[mu], new_v.at[mu], pc_sem.at[mu])
 
     load_piv.start()
-    for h in range(halves):
-        for mu in range(mu_dev):
-            load_prev(h, mu).start()
-    load_inv.start()
-
     barrier = pltpu.get_barrier_semaphore()
 
     @pl.loop(1, N)
@@ -73,10 +68,16 @@
             barrier, inc=1, device_id={"rows": peer // G, "grp": lax.rem(peer, G)}, device_id_type=MESH
         )
 
+    load_piv.wait()
+    for h in range(halves):
+        for mu in range(mu_dev):
+            load_prev(h, mu).start()
+    load_inv.start()
+
     lanes = piv_col.shape[1]
-    load_piv.wait()
     piv_col[...] = jnp.broadcast_to(piv_v[...], (lanes, p)).T
-    for mu in range(mu_dev):
+
+    def heat(mu):
         base = (r * mu_dev + mu) * (nu * G) + g * nu
 
         @pl.loop(0, nu // lanes)
@@ -99,6 +100,8 @@
 
         @pl.loop(0, mu_dev)
         def _(mu):
+            if h == 0:
+                heat(mu)
             load_prev(h, mu).wait()
             picked[...] += jnp.dot(hot_v[mu], prev_v[mu, :, h * kh : (h + 1) * kh], preferred_element_type=F32)
 
@@ -186,7 +189,7 @@
         take_rows(h)
 
     chunk = 512 if nu % 512 == 0 else 256
-    orders = group_orders(G)
+    orders, place = group_orders(G)
 
     def make_vectors(mu):
         load_pc(mu).wait()
@@ -201,9 +204,13 @@
         pltpu.make_async_copy(here, here, sem.at[slot, mu]).wait()
         block_v[...] += buf[slot, mu].astype(F32)
 
+    def hand_out(mu, src, dst, send, recv, grp):
+        for k in range(R):
+            peer = lax.rem(r + k, R)
+            remote(src.at[peer], dst.at[r * mu_dev + mu], send, recv, peer, grp).start()
+
     for s in range(G):
         to = choose(g, [order[s] for order in orders])
-        own = s == G - 1
 
         @pl.loop(0, mu_dev)
         def _(mu):
@@ -211,28 +218,41 @@
                 make_vectors(mu)
             at = pl.ds(pl.multiple_of(to * j_dev, j_dev), j_dev)
             block_v[...] = jnp.dot(orb_t[at, :], new_v[mu], preferred_element_type=F32)
-            if chained(G):
-                if G > 1:
-                    pl.when((to >= g) & (g > 0))(lambda: add(in_up, to, up_sem, mu))
-                    pl.when((to <= g) & (g < G - 1))(lambda: add(in_down, to, down_sem, mu))
-            elif own:
-                for d, q in grp_peers:
-                    add(in_up, q, up_sem, mu)
-            if own:
-                half = block_v[...].T.astype(BF16)
+            if s == place:
+                whole = block_v[...].T
                 for k in range(R):
-                    fin_v[mu, k] = half[k * c : (k + 1) * c, :]
+                    own_out[mu, k] = whole[k * c : (k + 1) * c, :]
+                own_in[r * mu_dev + mu] = own_out[mu, r]
+                for k in range(1, R):
+                    peer = lax.rem(r + k, R)
+                    remote(
+                        own_out.at[mu, peer], own_in.at[r * mu_dev + mu], own_send, own_recv, peer, g
+                    ).start()
+                return
+            if not chained(G):
+                turned = block_v[...].T.astype(BF16)
+                slot = s - (s > place)
                 for k in range(R):
-                    peer = lax.rem(r + k, R)
-                    src = fin_v.at[mu, peer]
-                    dst = out_hbm.at[r * mu_dev + mu]
-                    if k:
-                        remote(src, dst, send_sem, recv_sem, peer, g).start()
-                    else:
-                        pltpu.make_async_copy(src, dst, own_sem).start()
+                    last[slot, mu, k] = turned[k * c : (k + 1) * c, :]
+                hand_out(mu, last.at[slot, mu], last_in.at[g], last_send, last_recv.at[g], to)
                 return
-            send[to, mu] = block_v[...].astype(BF16)
-            if chained(G):
+            pl.when((to > g) & (g > 0))(lambda: add(in_up, to, up_sem, mu))
+            pl.when((to < g) & (g < G - 1))(lambda: add(in_down, to, down_sem, mu))
+            next_up = to == g + 1
+            next_down = to == g - 1
+
+            @pl.when(next_up | next_down)
+            def _():
+                slot = jnp.where(next_up, 0, 1)
+                turned = block_v[...].T.astype(BF16)
+                for k in range(R):
+                    last[slot, mu, k] = turned[k * c : (k + 1) * c, :]
+                hand_out(mu, last.at[slot, mu], last_in.at[slot], last_send, last_recv.at[slot], to)
+
+            @pl.when(jnp.logical_not(next_up | next_down))
+            def _():
+                send[to, mu] = block_v[...].astype(BF16)
+
                 @pl.when(to > g)
                 def _():
                     remote(send.at[to, mu], in_up.at[to, mu], hop_sem, up_sem.at[to, mu], r, g + 1).start()
@@ -240,21 +260,44 @@
                 @pl.when(to < g)
                 def _():
                     remote(send.at[to, mu], in_down.at[to, mu], hop_sem, down_sem.at[to, mu], r, g - 1).start()
-            else:
-                remote(send.at[to, mu], in_up.at[g, mu], hop_sem, up_sem.at[g, mu], r, to).start()
+
+    def take(copy, when):
+        pl.when(when)(copy.wait)
+
+    def gather(slot, when):
+        everything = last_in.at[slot]
+        take(pltpu.make_async_copy(everything, everything, last_recv.at[slot]), when)
+
+        @pl.when(when)
+        def _():
+            own_in[...] += last_in[slot].astype(F32)
+
+    others = own_in.at[pl.ds(0, (R - 1) * mu_dev)]
+    pltpu.make_async_copy(others, others, own_recv).wait()
+    if chained(G):
+        early = g >= G // 2
+        gather(0, (g > 0) & early)
+        gather(1, g < G - 1)
+        gather(0, (g > 0) & jnp.logical_not(early))
+    else:
+        for slot in range(G):
+            gather(slot, g != slot)
+    out_v[...] = own_in[...].astype(BF16)
 
     for h in range(halves):
         for copy in first(h) + second(h) + third(h):
             copy.wait_send()
-    own = out_hbm.at[pl.ds(0, mu_dev)]
-    pltpu.make_async_copy(own, own, own_sem).wait()
-    if G > 1:
-        hops = send.at[pl.ds(0, G - 1)]
-        pltpu.make_async_copy(hops, hops, hop_sem).wait()
-    if R > 1:
-        every = out_hbm.at[pl.ds(0, (R - 1) * mu_dev)]
-        pltpu.make_async_copy(every, every, send_sem).wait()
-        pltpu.make_async_copy(every, every, recv_sem).wait()
+    pltpu.make_async_copy(others, others, own_send).wait()
+    if chained(G):
+        ends = (g > 0).astype(jnp.int32) + (g < G - 1).astype(jnp.int32)
+        for count in range(1, 3):
+            near = last.at[pl.ds(0, count)]
+            take(pltpu.make_async_copy(near, near, last_send), ends == count)
+            if G - 1 > count:
+                far = send.at[pl.ds(0, G - 1 - count)]
+                take(pltpu.make_async_copy(far, far, hop_sem), ends == count)
+    else:
+        pltpu.make_async_copy(last, last, last_send).wait()
 
 
 def fused(pivots, columns, previous, inverse, orbitals, R, G):
@@ -265,17 +308,19 @@
     halves = 2
     kh = k // halves
     hbm = pl.BlockSpec(memory_space=pltpu.HBM)
-    anywhere = pl.BlockSpec(memory_space=pl.ANY)
+    slots = 2 if chained(G) else G
+    relays = G if chained(G) else 1
+    blocks = (R * mu_dev, c, nj // G)
     vmem = pl.BlockSpec(memory_space=pltpu.VMEM)
     dma = pltpu.SemaphoreType.DMA
     return pl.pallas_call(
         functools.partial(fused_kernel, R, G),
         out_shape=(
-            jax.ShapeDtypeStruct((R * mu_dev, c, nj // G), BF16),
+            jax.ShapeDtypeStruct(blocks, BF16),
             jax.ShapeDtypeStruct(columns.shape, BF16),
         ),
         in_specs=[hbm, hbm, hbm, hbm, hbm],
-        out_specs=(anywhere, vmem),
+        out_specs=(vmem, vmem),
         scratch_shapes=[
             pltpu.VMEM((1, p), jnp.int32),
             pltpu.VMEM((p, p), BF16),
@@ -292,13 +337,16 @@
             pltpu.VMEM((nu, nj), BF16),
             pltpu.VMEM((nj, nu), BF16),
             pltpu.VMEM((nj // G, p), F32),
-            pltpu.VMEM((G, mu_dev, nj // G, p), BF16),
-            pltpu.VMEM((G, mu_dev, nj // G, p), BF16),
-            pltpu.VMEM((G, mu_dev, nj // G, p), BF16),
-            pltpu.VMEM((mu_dev, R, c, nj // G), BF16),
+            pltpu.VMEM((relays, mu_dev, nj // G, p), BF16),
+            pltpu.VMEM((relays, mu_dev, nj // G, p), BF16),
+            pltpu.VMEM((relays, mu_dev, nj // G, p), BF16),
+            pltpu.VMEM((2 if chained(G) else G - 1, mu_dev, R, c, nj // G), BF16),
+            pltpu.VMEM((mu_dev, R, c, nj // G), F32),
+            pltpu.VMEM((slots,) + blocks, BF16),
+            pltpu.VMEM(blocks, F32),
             dma((halves, R)), dma((halves, R)), dma((halves, G)), dma((halves, G)), dma((halves, R)), dma((halves, R)),
             dma((2,)), dma((halves, mu_dev)), dma((mu_dev,)), dma(()),
-            dma(()), dma(()), dma((G, mu_dev)), dma((G, mu_dev)), dma(()), dma(()),
+            dma(()), dma((G, mu_dev)), dma((G, mu_dev)), dma(()), dma((slots,)), dma(()), dma(()),
         ],
         compiler_params=pltpu.CompilerParams(
             collective_id=0, has_side_effects=True, vmem_limit_bytes=44 * 1024 * 1024
@@ -307,34 +355,37 @@
     )(pivots, columns, previous, inverse, orbitals)
 
 
-def block_kernel(part_ref, slab_ref, made_ref, out_ref, new_hbm, part_v, spread_ref, new_sem):
-    mus, vecs, _ = part_ref.shape
-    groups, _, _, j = out_ref.shape
-    lot = vecs // groups
+def block_kernel(part_ref, slab_ref, made_ref, out_hbm, new_hbm, out_v, part_v, spread_ref, new_sem, out_sem):
+    mus, vecs, j = part_ref.shape
+    groups, lot, _, _ = out_v.shape
     wide = mus * lot
-    step = pl.program_id(0)
     store = pltpu.make_async_copy(made_ref, new_hbm, new_sem)
-
-    @pl.when(step == 0)
-    def _():
-        store.start()
-        mu = lax.broadcasted_iota(jnp.int32, (mus, wide), 0)
-        col = lax.broadcasted_iota(jnp.int32, (mus, wide), 1)
-        repeat = jnp.where(lax.shift_right_logical(col, lot.bit_length() - 1) == mu, 1.0, 0.0).astype(BF16)
-        spread_ref[...] = lax.dot_general(
-            slab_ref[...], repeat, (((0,), (0,)), ((), ())), preferred_element_type=F32
-        ).astype(BF16)
+    store.start()
+    mu = lax.broadcasted_iota(jnp.int32, (mus, wide), 0)
+    col = lax.broadcasted_iota(jnp.int32, (mus, wide), 1)
+    repeat = jnp.where(lax.shift_right_logical(col, lot.bit_length() - 1) == mu, 1.0, 0.0).astype(BF16)
+    spread_ref[...] = lax.dot_general(
+        slab_ref[...], repeat, (((0,), (0,)), ((), ())), preferred_element_type=F32
+    ).astype(BF16)
+    for k in range(groups):
+        part_v[k] = part_ref[:, k * lot : (k + 1) * lot, :].reshape(wide, j)
+
+    def piece(q, k):
+        return pltpu.make_async_copy(out_v.at[k, q], out_hbm.at[k, q], out_sem.at[k, q])
+
+    @pl.loop(0, lot)
+    def _(q):
+        at = lax.broadcasted_iota(jnp.int32, spread_ref.shape, 1) & (lot - 1)
+        kept = jnp.where(at == q, spread_ref[...].astype(F32), 0.0).astype(BF16)
         for k in range(groups):
-            part_v[:, k * j : (k + 1) * j] = part_ref[:, k * lot : (k + 1) * lot, :].reshape(wide, j)
-
-    col = lax.broadcasted_iota(jnp.int32, spread_ref.shape, 1) & (lot - 1)
-    kept = jnp.where(col == step, spread_ref[...].astype(F32), 0.0).astype(BF16)
-    for k in range(groups):
-        out_ref[k, 0] = jnp.dot(kept, part_v[:, k * j : (k + 1) * j], preferred_element_type=F32).astype(BF16)
-
-    @pl.when(step == pl.num_programs(0) - 1)
-    def _():
-        store.wait()
+            out_v[k, q] = jnp.dot(kept, part_v[k], preferred_element_type=F32).astype(BF16)
+            piece(q, k).start()
+
+    @pl.loop(0, lot)
+    def _(q):
+        for k in range(groups):
+            piece(q, k).wait()
+    store.wait()
 
 
 def orbital_block(part, slab, made):
@@ -342,25 +393,23 @@
     i = slab.shape[1]
     lot = 8
     assert vecs % lot == 0
+    groups = vecs // lot
+    vmem = pl.BlockSpec(memory_space=pltpu.VMEM)
+    anywhere = pl.BlockSpec(memory_space=pl.ANY)
     out, new = pl.pallas_call(
         block_kernel,
-        grid=(lot,),
         out_shape=(
-            jax.ShapeDtypeStruct((vecs // lot, lot, i, j), BF16),
+            jax.ShapeDtypeStruct((groups, lot, i, j), BF16),
             jax.ShapeDtypeStruct(made.shape, BF16),
         ),
-        in_specs=[
-            pl.BlockSpec(memory_space=pltpu.VMEM),
-            pl.BlockSpec((mus, i), lambda s: (0, 0)),
-            pl.BlockSpec(memory_space=pltpu.VMEM),
-        ],
-        out_specs=(
-            pl.BlockSpec((vecs // lot, 1, i, j), lambda s: (0, s, 0, 0)), pl.BlockSpec(memory_space=pl.ANY)
-        ),
+        in_specs=[vmem, vmem, vmem],
+        out_specs=(anywhere, anywhere),
         scratch_shapes=[
-            pltpu.VMEM((mus * lot, vecs // lot * j), BF16),
+            pltpu.VMEM((groups, lot, i, j), BF16),
+            pltpu.VMEM((groups, mus * lot, j), BF16),
             pltpu.VMEM((i, mus * lot), BF16),
             pltpu.SemaphoreType.DMA(()),
+            pltpu.SemaphoreType.DMA((groups, lot)),
         ],
         compiler_params=pltpu.CompilerParams(vmem_limit_bytes=40 * 1024 * 1024),
         name="orbital_block",

time: 75.3 us -> 74.1 us (0.984)
  Pallas kernels: 74.5 us -> 73.1 us
    pallas_call x1, Pallas kernels: 9.89 us -> 8.11 us  [orbital_block(): pl.pallas_call(block_kernel, out_shape=(jax.ShapeDtypeStruct((groups, lot...]
where the time goes in v3:
time: 74.1 us; the launch traced here: 73.7 us
  Pallas kernels  73.1 us (99%)
    pallas_call x1, Pallas kernels, fused(): pl.pallas_call(functools.partial(fused_kernel, R, G), out_shape=(jax.Shap...  65 us
    pallas_call x1, Pallas kernels, orbital_block(): pl.pallas_call(block_kernel, out_shape=(jax.ShapeDtypeStruct((groups, lot...  8.11 us

profile of v3, /device:TPU:9, one launch (start us, length us, event | category | flops | bytes accessed | tf_op | source)
XLA Modules:
  0.0 73.7 jit_solution(5492567884758810481)
XLA Ops:
  0.6 0.0 copy-start
  0.6 65.0 %fused_exchange.1 = (bf16[32,32,256]{2,1,0:T(8,128)(2,1)S(1)}, bf16[4,2560,256]{2,1,0:T(8,128)(2,1)S(1)}) custom-call(s32[1,256]{1,0:T(1,128)} %bitcast.2, bf16[4,2560,256]{2,1,0:T(8,128)(2,1)} %pc_hbm.1, bf16[4,2560,512]{2,1,0:T(8,128)(2,1)} %prev_hbm.1, bf16[256,256]{1,0:T(8,128)(2,1)} %inv_hbm.1, bf16[2560,1024]{1,0:T(8,128)(2,1)} %orb_hbm.1), custom_call_target="tpu_custom_call" | custom-call | tf_op jit(solution)/shard_map/fused_exchange/pallas_call | solution.py:316
  65.6 0.0 copy-done
  65.6 8.1 %orbital_block.1 = (bf16[4,8,1024,256]{3,2,1,0:T(8,128)(2,1)}, bf16[4,2560,256]{2,1,0:T(8,128)(2,1)}) custom-call(bf16[32,32,256]{2,1,0:T(8,128)(2,1)S(1)} %get-tuple-element.6.part_ref, bf16[32,1024]{1,0:T(8,128)(2,1)S(1)} %copy-done, bf16[4,2560,256]{2,1,0:T(8,128)(2,1)S(1)} %get-tuple-element.7.made_ref), custom_call_target="tpu_custom_call" | custom-call | tf_op jit(solution)/shard_map/orbital_block/pallas_call | solution.py:399
Async XLA Ops:
  0.6 65.0 %copy-start = (bf16[32,1024]{1,0:T(8,128)(2,1)S(1)}, bf16[32,1024]{1,0:T(8,128)(2,1)}, u32[]{:S(2)}) copy-start(bf16[32,1024]{1,0:T(8,128)(2,1)} %slab_ref.1) | copy-start | bytes 196612

commit v4 on v3

--- a/solution.py
+++ b/solution.py
@@ -18,11 +18,11 @@
 
 def group_orders(G):
     def due(g, d):
+        if d == g:
+            return 4 * G if chained(G) and g in (0, G - 1) else -1
         return 2 * (G - 1 - d) + g if d > g else 2 * d + G - 1 - g
 
-    place = max(G - 2, 0)
-    orders = [sorted((d for d in range(G) if d != g), key=lambda d: (due(g, d), d)) for g in range(G)]
-    return [order[:place] + [g] + order[place:] for g, order in enumerate(orders)], place
+    return [sorted(range(G), key=lambda d: (due(g, d), d)) for g in range(G)]
 
 
 def choose(g, values):
@@ -86,6 +86,9 @@
             at = lax.broadcasted_iota(jnp.int32, (p, lanes), 1) + (base + start)
             hot_v[mu, :, pl.ds(start, lanes)] = jnp.where(piv_col[...] == at, 1.0, 0.0).astype(BF16)
 
+    for mu in range(mu_dev):
+        heat(mu)
+
     def remote(src, dst, send, recv, row, grp):
         return pltpu.make_async_remote_copy(
             src_ref=src, dst_ref=dst, send_sem=send, recv_sem=recv,
@@ -100,8 +103,6 @@
 
         @pl.loop(0, mu_dev)
         def _(mu):
-            if h == 0:
-                heat(mu)
             load_prev(h, mu).wait()
             picked[...] += jnp.dot(hot_v[mu], prev_v[mu, :, h * kh : (h + 1) * kh], preferred_element_type=F32)
 
@@ -178,9 +179,10 @@
     low = lax.broadcasted_iota(jnp.int32, (p, p), 0)
     high = lax.broadcasted_iota(jnp.int32, (p, p), 1)
     upper_v[...] = jnp.where(low <= high, inv_v[...].astype(F32), 0.0).astype(BF16)
-    load_orb.wait()
     for h in range(halves):
         add_rows(h)
+        if h == 0:
+            load_orb.wait()
         turn_orbitals(cuts[h], cuts[h + 1])
     for h in range(halves):
         add_groups(h)
@@ -188,15 +190,17 @@
     for h in range(halves):
         take_rows(h)
 
-    chunk = 512 if nu % 512 == 0 else 256
-    orders, place = group_orders(G)
+    chunk = nu // 2
+    orders = group_orders(G)
 
     def make_vectors(mu):
         load_pc(mu).wait()
-        for i in range(nu // chunk):
-            at = pl.ds(i * chunk, chunk)
+        parts = [pl.ds(i * chunk, chunk) for i in range(nu // chunk)]
+        left = []
+        for at in parts:
             correction = jnp.dot(prev_v[mu, at, :], rows_t[...], preferred_element_type=F32)
-            residual = (new_v[mu, at, :].astype(F32) - correction).astype(BF16)
+            left.append((new_v[mu, at, :].astype(F32) - correction).astype(BF16))
+        for at, residual in zip(parts, left):
             new_v[mu, at, :] = jnp.dot(residual, upper_v[...], preferred_element_type=F32).astype(BF16)
 
     def add(buf, slot, sem, mu):
@@ -209,95 +213,140 @@
             peer = lax.rem(r + k, R)
             remote(src.at[peer], dst.at[r * mu_dev + mu], send, recv, peer, grp).start()
 
-    for s in range(G):
+    at_low = g == 0
+    at_high = g == G - 1
+    at_end = (at_low | at_high) & chained(G)
+
+    def emit(to, mu):
+        own = to == g
+        if chained(G):
+            pl.when(jnp.logical_not(at_low) & ((to > g) | (own & at_high)))(lambda: add(in_up, to, up_sem, mu))
+            pl.when(jnp.logical_not(at_high) & ((to < g) | (own & at_low)))(lambda: add(in_down, to, down_sem, mu))
+            near = ((to == g + 1) & (to < G - 1)) | ((to == g - 1) & (to > 0))
+        else:
+            near = jnp.logical_not(own)
+
+        @pl.when(own & jnp.logical_not(at_end))
+        def _():
+            whole = block_v[...].T
+            for k in range(R):
+                own_out[mu, k] = whole[k * c : (k + 1) * c, :]
+            own_in[r * mu_dev + mu] = own_out[mu, r]
+            for k in range(1, R):
+                peer = lax.rem(r + k, R)
+                remote(own_out.at[mu, peer], own_in.at[r * mu_dev + mu], own_send, own_recv, peer, g).start()
+
+        def turn_last(slot):
+            turned = block_v[...].T.astype(BF16)
+            for k in range(R):
+                last[slot, mu, k] = turned[k * c : (k + 1) * c, :]
+
+        @pl.when(near)
+        def _():
+            if chained(G):
+                slot = jnp.where(to > g, 0, 1)
+                into = slot
+            else:
+                slot = to - (to > g).astype(jnp.int32)
+                into = g
+            turn_last(slot)
+            for k in range(R):
+                peer = lax.rem(r + k, R)
+                remote(
+                    last.at[slot, mu, peer], last_in.at[into, r * mu_dev + mu], last_send, last_recv.at[into], peer, to
+                ).start()
+
+        if not chained(G):
+            return
+
+        @pl.when(own & at_end)
+        def _():
+            slot = jnp.where(at_low, 1, 0)
+            turn_last(slot)
+            last_in[0, r * mu_dev + mu] = last[slot, mu, r]
+            for k in range(1, R):
+                peer = lax.rem(r + k, R)
+                remote(
+                    last.at[slot, mu, peer], last_in.at[0, r * mu_dev + mu], own_send, last_recv.at[0], peer, g
+                ).start()
+
+        @pl.when(jnp.logical_not(own | near))
+        def _():
+            send[to, mu] = block_v[...].astype(BF16)
+
+            @pl.when(to > g)
+            def _():
+                remote(send.at[to, mu], in_up.at[to, mu], hop_sem, up_sem.at[to, mu], r, g + 1).start()
+
+            @pl.when(to < g)
+            def _():
+                remote(send.at[to, mu], in_down.at[to, mu], hop_sem, down_sem.at[to, mu], r, g - 1).start()
+
+    def block(to, mu):
+        at = pl.ds(pl.multiple_of(to * j_dev, j_dev), j_dev)
+        block_v[...] = jnp.dot(orb_t[at, :], new_v[mu], preferred_element_type=F32)
+
+    initial = choose(g, [order[0] for order in orders])
+
+    @pl.loop(0, mu_dev)
+    def _(mu):
+        make_vectors(mu)
+        block(initial, mu)
+        emit(initial, mu)
+
+    for s in range(1, G):
         to = choose(g, [order[s] for order in orders])
 
         @pl.loop(0, mu_dev)
         def _(mu):
-            if s == 0:
-                make_vectors(mu)
-            at = pl.ds(pl.multiple_of(to * j_dev, j_dev), j_dev)
-            block_v[...] = jnp.dot(orb_t[at, :], new_v[mu], preferred_element_type=F32)
-            if s == place:
-                whole = block_v[...].T
-                for k in range(R):
-                    own_out[mu, k] = whole[k * c : (k + 1) * c, :]
-                own_in[r * mu_dev + mu] = own_out[mu, r]
-                for k in range(1, R):
-                    peer = lax.rem(r + k, R)
-                    remote(
-                        own_out.at[mu, peer], own_in.at[r * mu_dev + mu], own_send, own_recv, peer, g
-                    ).start()
-                return
-            if not chained(G):
-                turned = block_v[...].T.astype(BF16)
-                slot = s - (s > place)
-                for k in range(R):
-                    last[slot, mu, k] = turned[k * c : (k + 1) * c, :]
-                hand_out(mu, last.at[slot, mu], last_in.at[g], last_send, last_recv.at[g], to)
-                return
-            pl.when((to > g) & (g > 0))(lambda: add(in_up, to, up_sem, mu))
-            pl.when((to < g) & (g < G - 1))(lambda: add(in_down, to, down_sem, mu))
-            next_up = to == g + 1
-            next_down = to == g - 1
-
-            @pl.when(next_up | next_down)
-            def _():
-                slot = jnp.where(next_up, 0, 1)
-                turned = block_v[...].T.astype(BF16)
-                for k in range(R):
-                    last[slot, mu, k] = turned[k * c : (k + 1) * c, :]
-                hand_out(mu, last.at[slot, mu], last_in.at[slot], last_send, last_recv.at[slot], to)
-
-            @pl.when(jnp.logical_not(next_up | next_down))
-            def _():
-                send[to, mu] = block_v[...].astype(BF16)
-
-                @pl.when(to > g)
-                def _():
-                    remote(send.at[to, mu], in_up.at[to, mu], hop_sem, up_sem.at[to, mu], r, g + 1).start()
-
-                @pl.when(to < g)
-                def _():
-                    remote(send.at[to, mu], in_down.at[to, mu], hop_sem, down_sem.at[to, mu], r, g - 1).start()
-
-    def take(copy, when):
-        pl.when(when)(copy.wait)
+            block(to, mu)
+            emit(to, mu)
+
+    def take(buf, sem, when):
+        pl.when(when)(pltpu.make_async_copy(buf, buf, sem).wait)
 
     def gather(slot, when):
-        everything = last_in.at[slot]
-        take(pltpu.make_async_copy(everything, everything, last_recv.at[slot]), when)
+        take(last_in.at[slot], last_recv.at[slot], when)
 
         @pl.when(when)
         def _():
             own_in[...] += last_in[slot].astype(F32)
 
+    inner = jnp.logical_not(at_end)
     others = own_in.at[pl.ds(0, (R - 1) * mu_dev)]
-    pltpu.make_async_copy(others, others, own_recv).wait()
+    take(others, own_recv, inner)
     if chained(G):
-        early = g >= G // 2
-        gather(0, (g > 0) & early)
-        gather(1, g < G - 1)
-        gather(0, (g > 0) & jnp.logical_not(early))
+        gather(0, inner & (2 * g >= G))
+        gather(1, inner)
+        gather(0, inner & (2 * g < G))
+        rounded = last_in.at[0, pl.ds(0, (R - 1) * mu_dev)]
+        take(rounded, last_recv.at[0], at_end)
+
+        @pl.when(at_end)
+        def _():
+            out_v[...] = last_in[0]
     else:
         for slot in range(G):
             gather(slot, g != slot)
-    out_v[...] = own_in[...].astype(BF16)
+
+    @pl.when(inner)
+    def _():
+        out_v[...] = own_in[...].astype(BF16)
 
     for h in range(halves):
         for copy in first(h) + second(h) + third(h):
             copy.wait_send()
-    pltpu.make_async_copy(others, others, own_send).wait()
+    take(others, own_send, inner)
     if chained(G):
-        ends = (g > 0).astype(jnp.int32) + (g < G - 1).astype(jnp.int32)
-        for count in range(1, 3):
-            near = last.at[pl.ds(0, count)]
-            take(pltpu.make_async_copy(near, near, last_send), ends == count)
+        take(rounded, own_send, at_end)
+        nears = (g + 1 < G - 1).astype(jnp.int32) + (g - 1 > 0).astype(jnp.int32)
+        for count in range(3):
+            if count:
+                take(last.at[pl.ds(0, count)], last_send, nears == count)
             if G - 1 > count:
-                far = send.at[pl.ds(0, G - 1 - count)]
-                take(pltpu.make_async_copy(far, far, hop_sem), ends == count)
+                take(send.at[pl.ds(0, G - 1 - count)], hop_sem, nears == count)
     else:
-        pltpu.make_async_copy(last, last, last_send).wait()
+        take(last, last_send, inner)
 
 
 def fused(pivots, columns, previous, inverse, orbitals, R, G):

time: 74.1 us -> 67.3 us (0.908)
  Pallas kernels: 73.1 us -> 66.5 us
    pallas_call x1, Pallas kernels: 65 us -> 58.4 us  [fused(): pl.pallas_call(functools.partial(fused_kernel, R, G), out_shape=(jax.Shap...]
where the time goes in v4:
time: 67.3 us; the launch traced here: 67.2 us
  Pallas kernels  66.5 us (99%)
    pallas_call x1, Pallas kernels, fused(): pl.pallas_call(functools.partial(fused_kernel, R, G), out_shape=(jax.Shap...  58.4 us
    pallas_call x1, Pallas kernels, orbital_block(): pl.pallas_call(block_kernel, out_shape=(jax.ShapeDtypeStruct((groups, lot...  8.11 us

profile of v4, /device:TPU:9, one launch (start us, length us, event | category | flops | bytes accessed | tf_op | source)
XLA Modules:
  0.0 67.2 jit_solution(11682865689736025830)
XLA Ops:
  0.6 0.0 copy-start
  0.6 58.4 %fused_exchange.1 = (bf16[32,32,256]{2,1,0:T(8,128)(2,1)S(1)}, bf16[4,2560,256]{2,1,0:T(8,128)(2,1)S(1)}) custom-call(s32[1,256]{1,0:T(1,128)} %bitcast.2, bf16[4,2560,256]{2,1,0:T(8,128)(2,1)} %pc_hbm.1, bf16[4,2560,512]{2,1,0:T(8,128)(2,1)} %prev_hbm.1, bf16[256,256]{1,0:T(8,128)(2,1)} %inv_hbm.1, bf16[2560,1024]{1,0:T(8,128)(2,1)} %orb_hbm.1), custom_call_target="tpu_custom_call" | custom-call | tf_op jit(solution)/shard_map/fused_exchange/pallas_call | solution.py:365
  59.1 0.0 copy-done
  59.1 8.1 %orbital_block.1 = (bf16[4,8,1024,256]{3,2,1,0:T(8,128)(2,1)}, bf16[4,2560,256]{2,1,0:T(8,128)(2,1)}) custom-call(bf16[32,32,256]{2,1,0:T(8,128)(2,1)S(1)} %get-tuple-element.6.part_ref, bf16[32,1024]{1,0:T(8,128)(2,1)S(1)} %copy-done, bf16[4,2560,256]{2,1,0:T(8,128)(2,1)S(1)} %get-tuple-element.7.made_ref), custom_call_target="tpu_custom_call" | custom-call | tf_op jit(solution)/shard_map/orbital_block/pallas_call | solution.py:448
Async XLA Ops:
  0.6 58.4 %copy-start = (bf16[32,1024]{1,0:T(8,128)(2,1)S(1)}, bf16[32,1024]{1,0:T(8,128)(2,1)}, u32[]{:S(2)}) copy-start(bf16[32,1024]{1,0:T(8,128)(2,1)} %slab_ref.1) | copy-start | bytes 196612

commit v5 on v4

--- a/solution.py
+++ b/solution.py
@@ -35,14 +35,12 @@
 def fused_kernel(
     R, G, piv_hbm, pc_hbm, prev_hbm, inv_hbm, orb_hbm, out_v, new_v,
     piv_v, inv_v, piv_col, hot_v, picked, buf_x, buf_a, buf_b, buf_c, rows_t, upper_v, prev_v, orb_v, orb_t,
-    block_v, send, in_up, in_down, last, own_out, last_in, own_in,
+    block_v, begun, send, in_up, in_down, last, own_out, last_in, own_in,
     send_a, recv_a, send_b, recv_b, send_c, recv_c, small_sem, prev_sem, pc_sem, orb_sem,
     hop_sem, up_sem, down_sem, last_send, last_recv, own_send, own_recv,
 ):
     r = lax.axis_index("rows")
     g = lax.axis_index("grp")
-    N = R * G
-    me = r * G + g
     mu_dev, nu, p = new_v.shape
     _, _, j_dev, _ = send.shape
     halves, _, c, kh = buf_c.shape
@@ -61,33 +59,41 @@
     load_piv.start()
     barrier = pltpu.get_barrier_semaphore()
 
-    @pl.loop(1, N)
-    def _(d):
-        peer = lax.rem(me + d, N)
-        pl.semaphore_signal(
-            barrier, inc=1, device_id={"rows": peer // G, "grp": lax.rem(peer, G)}, device_id_type=MESH
-        )
-
-    load_piv.wait()
+    def greet(row, grp):
+        pl.semaphore_signal(barrier, inc=1, device_id={"rows": row, "grp": grp}, device_id_type=MESH)
+
+    def greet_rows(step):
+        @pl.loop(1, R)
+        def _(d):
+            greet(lax.rem(r + d, R), lax.rem(g + step + G, G))
+
+    greet_rows(0)
+    for d in range(1, G):
+        greet(r, lax.rem(g + d, G))
+    if chained(G):
+        if G > 1:
+            pl.when(g > 0)(lambda: greet_rows(-1))
+            pl.when(g < G - 1)(lambda: greet_rows(1))
+        sides = (g > 0).astype(jnp.int32) + (g < G - 1).astype(jnp.int32)
+    else:
+        for d in range(1, G):
+            greet_rows(d)
+        sides = G - 1
+    greetings = (sides + 1) * (R - 1) + G - 1
     for h in range(halves):
         for mu in range(mu_dev):
             load_prev(h, mu).start()
     load_inv.start()
+    load_piv.wait()
 
     lanes = piv_col.shape[1]
     piv_col[...] = jnp.broadcast_to(piv_v[...], (lanes, p)).T
 
     def heat(mu):
         base = (r * mu_dev + mu) * (nu * G) + g * nu
-
-        @pl.loop(0, nu // lanes)
-        def _(i):
-            start = pl.multiple_of(i * lanes, lanes)
-            at = lax.broadcasted_iota(jnp.int32, (p, lanes), 1) + (base + start)
-            hot_v[mu, :, pl.ds(start, lanes)] = jnp.where(piv_col[...] == at, 1.0, 0.0).astype(BF16)
-
-    for mu in range(mu_dev):
-        heat(mu)
+        for i in range(nu // lanes):
+            at = lax.broadcasted_iota(jnp.int32, (p, lanes), 1) + (base + i * lanes)
+            hot_v[mu, :, i * lanes : (i + 1) * lanes] = jnp.where(piv_col[...] == at, 1.0, 0.0).astype(BF16)
 
     def remote(src, dst, send, recv, row, grp):
         return pltpu.make_async_remote_copy(
@@ -97,6 +103,9 @@
 
     row_peers = [(d, lax.rem(r + d, R)) for d in range(1, R)]
     grp_peers = [(d, lax.rem(g + d, G)) for d in range(1, G)]
+
+    for mu in range(mu_dev):
+        heat(mu)
 
     def pick(h):
         picked[...] = jnp.zeros(picked.shape, F32)
@@ -148,6 +157,9 @@
         for k in range(R):
             picked[k * c : (k + 1) * c, :] = buf_c[h, k].astype(F32)
         rows_t[h * kh : (h + 1) * kh, :] = picked[...].T.astype(BF16)
+        if h == 0:
+            for at in parts:
+                begun[at, :] = jnp.dot(prev_v[0, at, :kh], rows_t[:kh, :], preferred_element_type=F32)
 
     square = (256, 256)
     eye = jnp.where(
@@ -172,7 +184,7 @@
             load_orb.start()
             for mu in range(mu_dev):
                 load_pc(mu).start()
-            pl.semaphore_wait(barrier, N - 1)
+            pl.semaphore_wait(barrier, greetings)
         for copy in first(h):
             copy.start()
     load_inv.wait()
@@ -187,18 +199,22 @@
     for h in range(halves):
         add_groups(h)
         turn_orbitals(cuts[halves + h], cuts[halves + h + 1])
+    chunk = nu // 2
+    parts = [pl.ds(i * chunk, chunk) for i in range(nu // chunk)]
     for h in range(halves):
         take_rows(h)
 
-    chunk = nu // 2
     orders = group_orders(G)
+    first_mu = 0
 
     def make_vectors(mu):
         load_pc(mu).wait()
-        parts = [pl.ds(i * chunk, chunk) for i in range(nu // chunk)]
         left = []
         for at in parts:
-            correction = jnp.dot(prev_v[mu, at, :], rows_t[...], preferred_element_type=F32)
+            if mu is first_mu:
+                correction = begun[at, :] + jnp.dot(prev_v[mu, at, kh:], rows_t[kh:, :], preferred_element_type=F32)
+            else:
+                correction = jnp.dot(prev_v[mu, at, :], rows_t[...], preferred_element_type=F32)
             left.append((new_v[mu, at, :].astype(F32) - correction).astype(BF16))
         for at, residual in zip(parts, left):
             new_v[mu, at, :] = jnp.dot(residual, upper_v[...], preferred_element_type=F32).astype(BF16)
@@ -288,7 +304,11 @@
 
     initial = choose(g, [order[0] for order in orders])
 
-    @pl.loop(0, mu_dev)
+    make_vectors(first_mu)
+    block(initial, first_mu)
+    emit(initial, first_mu)
+
+    @pl.loop(1, mu_dev)
     def _(mu):
         make_vectors(mu)
         block(initial, mu)
@@ -386,6 +406,7 @@
             pltpu.VMEM((nu, nj), BF16),
             pltpu.VMEM((nj, nu), BF16),
             pltpu.VMEM((nj // G, p), F32),
+            pltpu.VMEM((nu, p), F32),
             pltpu.VMEM((relays, mu_dev, nj // G, p), BF16),
             pltpu.VMEM((relays, mu_dev, nj // G, p), BF16),
             pltpu.VMEM((relays, mu_dev, nj // G, p), BF16),

time: 67.3 us -> 66.9 us (level)
  no operation moved by 1% of the time
where the time goes in v5:
time: 66.9 us; the launch traced here: 66.8 us
  Pallas kernels  66.1 us (99%)
    pallas_call x1, Pallas kernels, fused(): pl.pallas_call(functools.partial(fused_kernel, R, G), out_shape=(jax.Shap...  58 us
    pallas_call x1, Pallas kernels, orbital_block(): pl.pallas_call(block_kernel, out_shape=(jax.ShapeDtypeStruct((groups, lot...  8.11 us

profile of v5, /device:TPU:9, one launch (start us, length us, event | category | flops | bytes accessed | tf_op | source)
XLA Modules:
  0.0 66.8 jit_solution(13283075354331102407)
XLA Ops:
  0.6 0.0 copy-start
  0.6 58.0 %fused_exchange.1 = (bf16[32,32,256]{2,1,0:T(8,128)(2,1)S(1)}, bf16[4,2560,256]{2,1,0:T(8,128)(2,1)S(1)}) custom-call(s32[1,256]{1,0:T(1,128)} %bitcast.2, bf16[4,2560,256]{2,1,0:T(8,128)(2,1)} %pc_hbm.1, bf16[4,2560,512]{2,1,0:T(8,128)(2,1)} %prev_hbm.1, bf16[256,256]{1,0:T(8,128)(2,1)} %inv_hbm.1, bf16[2560,1024]{1,0:T(8,128)(2,1)} %orb_hbm.1), custom_call_target="tpu_custom_call" | custom-call | tf_op jit(solution)/shard_map/fused_exchange/pallas_call | solution.py:385
  58.7 0.0 copy-done
  58.7 8.1 %orbital_block.1 = (bf16[4,8,1024,256]{3,2,1,0:T(8,128)(2,1)}, bf16[4,2560,256]{2,1,0:T(8,128)(2,1)}) custom-call(bf16[32,32,256]{2,1,0:T(8,128)(2,1)S(1)} %get-tuple-element.6.part_ref, bf16[32,1024]{1,0:T(8,128)(2,1)S(1)} %copy-done, bf16[4,2560,256]{2,1,0:T(8,128)(2,1)S(1)} %get-tuple-element.7.made_ref), custom_call_target="tpu_custom_call" | custom-call | tf_op jit(solution)/shard_map/orbital_block/pallas_call | solution.py:469
Async XLA Ops:
  0.6 58.0 %copy-start = (bf16[32,1024]{1,0:T(8,128)(2,1)S(1)}, bf16[32,1024]{1,0:T(8,128)(2,1)}, u32[]{:S(2)}) copy-start(bf16[32,1024]{1,0:T(8,128)(2,1)} %slab_ref.1) | copy-start | bytes 196612

commit v6 on v5

--- a/solution.py
+++ b/solution.py
@@ -35,15 +35,17 @@
 def fused_kernel(
     R, G, piv_hbm, pc_hbm, prev_hbm, inv_hbm, orb_hbm, out_v, new_v,
     piv_v, inv_v, piv_col, hot_v, picked, buf_x, buf_a, buf_b, buf_c, rows_t, upper_v, prev_v, orb_v, orb_t,
-    block_v, begun, send, in_up, in_down, last, own_out, last_in, own_in,
-    send_a, recv_a, send_b, recv_b, send_c, recv_c, small_sem, prev_sem, pc_sem, orb_sem,
-    hop_sem, up_sem, down_sem, last_send, last_recv, own_send, own_recv,
+    block_v, begun, send, relay_in, last, own_out, last_in, own_in,
+    rows_send, recv_a, recv_b, recv_c, small_sem, prev_sem, pc_sem, orb_sem,
+    hop_sem, relay_sem, last_send, last_recv, own_send, own_recv,
 ):
     r = lax.axis_index("rows")
     g = lax.axis_index("grp")
     mu_dev, nu, p = new_v.shape
     _, _, j_dev, _ = send.shape
-    halves, _, c, kh = buf_c.shape
+    _, c, k_all = buf_c.shape
+    halves = 2
+    kh = k_all // halves
 
     load_piv = pltpu.make_async_copy(piv_hbm, piv_v, small_sem.at[0])
     load_inv = pltpu.make_async_copy(inv_hbm, inv_v, small_sem.at[1])
@@ -104,8 +106,7 @@
     row_peers = [(d, lax.rem(r + d, R)) for d in range(1, R)]
     grp_peers = [(d, lax.rem(g + d, G)) for d in range(1, G)]
 
-    for mu in range(mu_dev):
-        heat(mu)
+    pl.loop(0, mu_dev)(heat)
 
     def pick(h):
         picked[...] = jnp.zeros(picked.shape, F32)
@@ -116,50 +117,52 @@
             picked[...] += jnp.dot(hot_v[mu], prev_v[mu, :, h * kh : (h + 1) * kh], preferred_element_type=F32)
 
         for k in range(R):
-            buf_x[h, k] = picked[k * c : (k + 1) * c, :].astype(BF16)
-
-    def first(h):
+            buf_x[k, :, h * kh : (h + 1) * kh] = picked[k * c : (k + 1) * c, :].astype(BF16)
+
+    def first(cols, n):
         return [
-            remote(buf_x.at[h, q], buf_a.at[h, d], send_a.at[h, d], recv_a.at[h, d], q, g) for d, q in row_peers
+            remote(buf_x.at[q, :, cols], buf_a.at[d, :, cols], rows_send, recv_a.at[n], q, g) for d, q in row_peers
         ]
 
-    def second(h):
+    def second(cols, n):
         return [
-            remote(buf_b.at[h, 0], buf_b.at[h, d], send_b.at[h, d], recv_b.at[h, d], r, q) for d, q in grp_peers
+            remote(buf_b.at[0, :, cols], buf_b.at[d, :, cols], rows_send, recv_b.at[n], r, q) for d, q in grp_peers
         ]
 
-    def third(h):
+    def third(cols, n):
         return [
-            remote(buf_c.at[h, r], buf_c.at[h, r], send_c.at[h, d], recv_c.at[h, d], q, g) for d, q in row_peers
+            remote(buf_c.at[r, :, cols], buf_c.at[r, :, cols], rows_send, recv_c.at[n], q, g) for d, q in row_peers
         ]
 
-    def add_rows(h):
-        total = buf_x[h, r].astype(F32)
-        for (d, _), copy in zip(row_peers, first(h)):
-            copy.wait_recv()
-            total = total + buf_a[h, d].astype(F32)
-        buf_b[h, 0] = total.astype(BF16)
-        for copy in second(h):
+    def wait_all(buf, count, cols, sem):
+        if count:
+            received = buf.at[pl.ds(0, count), :, cols]
+            pltpu.make_async_copy(received, received, sem).wait()
+
+    def add_rows(cols, n):
+        total = buf_x[r, :, cols].astype(F32)
+        wait_all(buf_a, R - 1, cols, recv_a.at[n])
+        for d, _ in row_peers:
+            total = total + buf_a[d, :, cols].astype(F32)
+        buf_b[0, :, cols] = total.astype(BF16)
+        for copy in second(cols, n):
             copy.start()
 
-    def add_groups(h):
-        total = buf_b[h, 0].astype(F32)
-        for (d, _), copy in zip(grp_peers, second(h)):
-            copy.wait_recv()
-            total = total + buf_b[h, d].astype(F32)
-        buf_c[h, r] = total.astype(BF16)
-        for copy in third(h):
+    def add_groups(cols, n):
+        total = buf_b[0, :, cols].astype(F32)
+        wait_all(buf_b, G - 1, cols, recv_b.at[n])
+        for d, _ in grp_peers:
+            total = total + buf_b[d, :, cols].astype(F32)
+        buf_c[r, :, cols] = total.astype(BF16)
+        for copy in third(cols, n):
             copy.start()
 
-    def take_rows(h):
-        for copy in third(h):
-            copy.wait_recv()
-        for k in range(R):
-            picked[k * c : (k + 1) * c, :] = buf_c[h, k].astype(F32)
-        rows_t[h * kh : (h + 1) * kh, :] = picked[...].T.astype(BF16)
-        if h == 0:
+    def take_rows(cols, n):
+        wait_all(buf_c, R - 1, cols, recv_c.at[n])
+        rows_t[cols, :] = buf_c[:, :, cols].reshape(p, cols.size).astype(F32).T.astype(BF16)
+        if n == 0:
             for at in parts:
-                begun[at, :] = jnp.dot(prev_v[0, at, :kh], rows_t[:kh, :], preferred_element_type=F32)
+                begun[at, :] = jnp.dot(prev_v[0, at, cols], rows_t[cols, :], preferred_element_type=F32)
 
     square = (256, 256)
     eye = jnp.where(
@@ -176,8 +179,10 @@
                     eye, orb_v[at, q * 256 : (q + 1) * 256], (((1,), (1,)), ((), ())), preferred_element_type=F32
                 ).astype(BF16)
 
+    parted = kh // 2 if kh % 256 == 0 else kh
+    pieces = [pl.ds(0, kh)] + [pl.ds(kh + at, parted) for at in range(0, kh, parted)]
     tiles = nu // 256
-    cuts = [tiles * k // (2 * halves) for k in range(2 * halves + 1)]
+    cuts = [0, tiles // 2, tiles * 4 // 5, tiles]
     for h in range(halves):
         pick(h)
         if h == 0:
@@ -185,24 +190,29 @@
             for mu in range(mu_dev):
                 load_pc(mu).start()
             pl.semaphore_wait(barrier, greetings)
-        for copy in first(h):
-            copy.start()
+        for n, cols in enumerate(pieces):
+            if (n > 0) == (h > 0):
+                for copy in first(cols, n):
+                    copy.start()
     load_inv.wait()
     low = lax.broadcasted_iota(jnp.int32, (p, p), 0)
     high = lax.broadcasted_iota(jnp.int32, (p, p), 1)
     upper_v[...] = jnp.where(low <= high, inv_v[...].astype(F32), 0.0).astype(BF16)
-    for h in range(halves):
-        add_rows(h)
-        if h == 0:
+    for n, cols in enumerate(pieces):
+        add_rows(cols, n)
+        if n == 0:
             load_orb.wait()
-        turn_orbitals(cuts[h], cuts[h + 1])
-    for h in range(halves):
-        add_groups(h)
-        turn_orbitals(cuts[halves + h], cuts[halves + h + 1])
+            turn_orbitals(cuts[0], cuts[1])
+    turn_orbitals(cuts[1], cuts[2])
+    for n, cols in enumerate(pieces):
+        add_groups(cols, n)
+        if n == 0:
+            turn_orbitals(cuts[2], cuts[3])
+
     chunk = nu // 2
     parts = [pl.ds(i * chunk, chunk) for i in range(nu // chunk)]
-    for h in range(halves):
-        take_rows(h)
+    for n, cols in enumerate(pieces):
+        take_rows(cols, n)
 
     orders = group_orders(G)
     first_mu = 0
@@ -219,15 +229,17 @@
         for at, residual in zip(parts, left):
             new_v[mu, at, :] = jnp.dot(residual, upper_v[...], preferred_element_type=F32).astype(BF16)
 
-    def add(buf, slot, sem, mu):
-        here = buf.at[slot, mu]
-        pltpu.make_async_copy(here, here, sem.at[slot, mu]).wait()
-        block_v[...] += buf[slot, mu].astype(F32)
-
-    def hand_out(mu, src, dst, send, recv, grp):
-        for k in range(R):
-            peer = lax.rem(r + k, R)
-            remote(src.at[peer], dst.at[r * mu_dev + mu], send, recv, peer, grp).start()
+    def add(slot, mu):
+        here = relay_in.at[slot, mu]
+        pltpu.make_async_copy(here, here, relay_sem.at[slot, mu]).wait()
+        block_v[...] += relay_in[slot, mu].astype(F32)
+
+    if R & (R - 1) == 0:
+        bits = [1 << b for b in range(R.bit_length() - 1)]
+        flips = [(b, b - 2 * b * lax.rem(r // b, 2)) for b in bits]
+        everyone = [r + sum(change for b, change in flips if m & b) for m in range(R - 1, -1, -1)]
+    else:
+        everyone = [lax.rem(r + k, R) for k in range(R - 1, -1, -1)]
 
     at_low = g == 0
     at_high = g == G - 1
@@ -236,8 +248,9 @@
     def emit(to, mu):
         own = to == g
         if chained(G):
-            pl.when(jnp.logical_not(at_low) & ((to > g) | (own & at_high)))(lambda: add(in_up, to, up_sem, mu))
-            pl.when(jnp.logical_not(at_high) & ((to < g) | (own & at_low)))(lambda: add(in_down, to, down_sem, mu))
+            from_low = jnp.logical_not(at_low) & ((to > g) | (own & at_high))
+            from_high = jnp.logical_not(at_high) & ((to < g) | (own & at_low))
+            pl.when(from_low | from_high)(lambda: add(to, mu))
             near = ((to == g + 1) & (to < G - 1)) | ((to == g - 1) & (to > 0))
         else:
             near = jnp.logical_not(own)
@@ -248,8 +261,7 @@
             for k in range(R):
                 own_out[mu, k] = whole[k * c : (k + 1) * c, :]
             own_in[r * mu_dev + mu] = own_out[mu, r]
-            for k in range(1, R):
-                peer = lax.rem(r + k, R)
+            for peer in everyone[:-1]:
                 remote(own_out.at[mu, peer], own_in.at[r * mu_dev + mu], own_send, own_recv, peer, g).start()
 
         def turn_last(slot):
@@ -266,8 +278,7 @@
                 slot = to - (to > g).astype(jnp.int32)
                 into = g
             turn_last(slot)
-            for k in range(R):
-                peer = lax.rem(r + k, R)
+            for peer in everyone:
                 remote(
                     last.at[slot, mu, peer], last_in.at[into, r * mu_dev + mu], last_send, last_recv.at[into], peer, to
                 ).start()
@@ -280,8 +291,7 @@
             slot = jnp.where(at_low, 1, 0)
             turn_last(slot)
             last_in[0, r * mu_dev + mu] = last[slot, mu, r]
-            for k in range(1, R):
-                peer = lax.rem(r + k, R)
+            for peer in everyone[:-1]:
                 remote(
                     last.at[slot, mu, peer], last_in.at[0, r * mu_dev + mu], own_send, last_recv.at[0], peer, g
                 ).start()
@@ -290,13 +300,8 @@
         def _():
             send[to, mu] = block_v[...].astype(BF16)
 
-            @pl.when(to > g)
-            def _():
-                remote(send.at[to, mu], in_up.at[to, mu], hop_sem, up_sem.at[to, mu], r, g + 1).start()
-
-            @pl.when(to < g)
-            def _():
-                remote(send.at[to, mu], in_down.at[to, mu], hop_sem, down_sem.at[to, mu], r, g - 1).start()
+            via = jnp.where(to > g, g + 1, g - 1)
+            remote(send.at[to, mu], relay_in.at[to, mu], hop_sem, relay_sem.at[to, mu], r, via).start()
 
     def block(to, mu):
         at = pl.ds(pl.multiple_of(to * j_dev, j_dev), j_dev)
@@ -353,9 +358,10 @@
     def _():
         out_v[...] = own_in[...].astype(BF16)
 
-    for h in range(halves):
-        for copy in first(h) + second(h) + third(h):
-            copy.wait_send()
+    every = pl.ds(0, k_all)
+    wait_all(buf_a, R - 1, every, rows_send)
+    wait_all(buf_b, G - 1, every, rows_send)
+    wait_all(buf_c, R - 1, every, rows_send)
     take(others, own_send, inner)
     if chained(G):
         take(rounded, own_send, at_end)
@@ -396,10 +402,10 @@
             pltpu.VMEM((p, 128), jnp.int32),
             pltpu.VMEM((mu_dev, p, nu), BF16),
             pltpu.VMEM((p, kh), F32),
-            pltpu.VMEM((halves, R, c, kh), BF16),
-            pltpu.VMEM((halves, R, c, kh), BF16),
-            pltpu.VMEM((halves, G, c, kh), BF16),
-            pltpu.VMEM((halves, R, c, kh), BF16),
+            pltpu.VMEM((R, c, k), BF16),
+            pltpu.VMEM((R, c, k), BF16),
+            pltpu.VMEM((G, c, k), BF16),
+            pltpu.VMEM((R, c, k), BF16),
             pltpu.VMEM((k, p), BF16),
             pltpu.VMEM((p, p), BF16),
             pltpu.VMEM((mu_dev, nu, k), BF16),
@@ -409,14 +415,12 @@
             pltpu.VMEM((nu, p), F32),
             pltpu.VMEM((relays, mu_dev, nj // G, p), BF16),
             pltpu.VMEM((relays, mu_dev, nj // G, p), BF16),
-            pltpu.VMEM((relays, mu_dev, nj // G, p), BF16),
             pltpu.VMEM((2 if chained(G) else G - 1, mu_dev, R, c, nj // G), BF16),
             pltpu.VMEM((mu_dev, R, c, nj // G), F32),
             pltpu.VMEM((slots,) + blocks, BF16),
             pltpu.VMEM(blocks, F32),
-            dma((halves, R)), dma((halves, R)), dma((halves, G)), dma((halves, G)), dma((halves, R)), dma((halves, R)),
-            dma((2,)), dma((halves, mu_dev)), dma((mu_dev,)), dma(()),
-            dma(()), dma((G, mu_dev)), dma((G, mu_dev)), dma(()), dma((slots,)), dma(()), dma(()),
+            dma(()), dma((halves + 1,)), dma((halves + 1,)), dma((halves + 1,)), dma((2,)), dma((halves, mu_dev)), dma((mu_dev,)), dma(()),
+            dma(()), dma((relays, mu_dev)), dma(()), dma((slots,)), dma(()), dma(()),
         ],
         compiler_params=pltpu.CompilerParams(
             collective_id=0, has_side_effects=True, vmem_limit_bytes=44 * 1024 * 1024
@@ -441,7 +445,7 @@
         part_v[k] = part_ref[:, k * lot : (k + 1) * lot, :].reshape(wide, j)
 
     def piece(q, k):
-        return pltpu.make_async_copy(out_v.at[k, q], out_hbm.at[k, q], out_sem.at[k, q])
+        return pltpu.make_async_copy(out_v.at[k, q], out_hbm.at[k, q], out_sem)
 
     @pl.loop(0, lot)
     def _(q):
@@ -451,10 +455,7 @@
             out_v[k, q] = jnp.dot(kept, part_v[k], preferred_element_type=F32).astype(BF16)
             piece(q, k).start()
 
-    @pl.loop(0, lot)
-    def _(q):
-        for k in range(groups):
-            piece(q, k).wait()
+    pltpu.make_async_copy(out_v, out_hbm, out_sem).wait()
     store.wait()
 
 
@@ -479,7 +480,7 @@
             pltpu.VMEM((groups, mus * lot, j), BF16),
             pltpu.VMEM((i, mus * lot), BF16),
             pltpu.SemaphoreType.DMA(()),
-            pltpu.SemaphoreType.DMA((groups, lot)),
+            pltpu.SemaphoreType.DMA(()),
         ],
         compiler_params=pltpu.CompilerParams(vmem_limit_bytes=40 * 1024 * 1024),
         name="orbital_block",

time: 66.9 us -> 65 us (0.972)
  Pallas kernels: 66.1 us -> 63.9 us
    pallas_call x1, Pallas kernels: 58 us -> 56.1 us  [fused(): pl.pallas_call(functools.partial(fused_kernel, R, G), out_shape=(jax.Shap...]
where the time goes in v6:
time: 65 us; the launch traced here: 64.5 us
  Pallas kernels  63.9 us (98%)
  between operations  0.66 us (1%)
    pallas_call x1, Pallas kernels, fused(): pl.pallas_call(functools.partial(fused_kernel, R, G), out_shape=(jax.Shap...  56.1 us
    pallas_call x1, Pallas kernels, orbital_block(): pl.pallas_call(block_kernel, out_shape=(jax.ShapeDtypeStruct((groups, lot...  7.79 us

profile of v6, /device:TPU:9, one launch (start us, length us, event | category | flops | bytes accessed | tf_op | source)
XLA Modules:
  0.0 64.5 jit_solution(10119355309274309569)
XLA Ops:
  0.6 0.0 copy-start
  0.6 56.1 %fused_exchange.1 = (bf16[32,32,256]{2,1,0:T(8,128)(2,1)S(1)}, bf16[4,2560,256]{2,1,0:T(8,128)(2,1)S(1)}) custom-call(s32[1,256]{1,0:T(1,128)} %bitcast.2, bf16[4,2560,256]{2,1,0:T(8,128)(2,1)} %pc_hbm.1, bf16[4,2560,512]{2,1,0:T(8,128)(2,1)} %prev_hbm.1, bf16[256,256]{1,0:T(8,128)(2,1)} %inv_hbm.1, bf16[2560,1024]{1,0:T(8,128)(2,1)} %orb_hbm.1), custom_call_target="tpu_custom_call" | custom-call | tf_op jit(solution)/shard_map/fused_exchange/pallas_call | solution.py:391
  56.7 0.0 copy-done
  56.7 7.8 %orbital_block.1 = (bf16[4,8,1024,256]{3,2,1,0:T(8,128)(2,1)}, bf16[4,2560,256]{2,1,0:T(8,128)(2,1)}) custom-call(bf16[32,32,256]{2,1,0:T(8,128)(2,1)S(1)} %get-tuple-element.6.part_ref, bf16[32,1024]{1,0:T(8,128)(2,1)S(1)} %copy-done, bf16[4,2560,256]{2,1,0:T(8,128)(2,1)S(1)} %get-tuple-element.7.made_ref), custom_call_target="tpu_custom_call" | custom-call | tf_op jit(solution)/shard_map/orbital_block/pallas_call | solution.py:470
Async XLA Ops:
  0.6 56.1 %copy-start = (bf16[32,1024]{1,0:T(8,128)(2,1)S(1)}, bf16[32,1024]{1,0:T(8,128)(2,1)}, u32[]{:S(2)}) copy-start(bf16[32,1024]{1,0:T(8,128)(2,1)} %slab_ref.1) | copy-start | bytes 196612

commit v7 on v6

--- a/solution.py
+++ b/solution.py
@@ -103,8 +103,17 @@
             device_id={"rows": row, "grp": grp}, device_id_type=MESH,
         )
 
-    row_peers = [(d, lax.rem(r + d, R)) for d in range(1, R)]
-    grp_peers = [(d, lax.rem(g + d, G)) for d in range(1, G)]
+    if R & (R - 1) == 0:
+        bits = [1 << b for b in range(R.bit_length() - 1)]
+        flips = [(b, b - 2 * b * lax.rem(r // b, 2)) for b in bits]
+        everyone = [r + sum(change for b, change in flips if m & b) for m in range(R - 1, -1, -1)]
+        row_peers = [(R - 1 - k, q) for k, q in enumerate(everyone[:-1])]
+    else:
+        everyone = [lax.rem(r + k, R) for k in range(R - 1, -1, -1)]
+        row_peers = [(R - 1 - k, q) for k, q in enumerate(everyone[:-1])]
+
+    turns = [jnp.where(2 * g < G, G - d, d) for d in range(1, G)]
+    grp_peers = [(d, lax.rem(g + d, G)) for d in turns]
 
     pl.loop(0, mu_dev)(heat)
 
@@ -234,16 +243,13 @@
         pltpu.make_async_copy(here, here, relay_sem.at[slot, mu]).wait()
         block_v[...] += relay_in[slot, mu].astype(F32)
 
-    if R & (R - 1) == 0:
-        bits = [1 << b for b in range(R.bit_length() - 1)]
-        flips = [(b, b - 2 * b * lax.rem(r // b, 2)) for b in bits]
-        everyone = [r + sum(change for b, change in flips if m & b) for m in range(R - 1, -1, -1)]
-    else:
-        everyone = [lax.rem(r + k, R) for k in range(R - 1, -1, -1)]
-
     at_low = g == 0
     at_high = g == G - 1
     at_end = (at_low | at_high) & chained(G)
+
+    def hop(to, at, sem):
+        via = jnp.where(to > g, g + 1, g - 1)
+        remote(send.at[at], relay_in.at[at], hop_sem, relay_sem.at[sem], r, via).start()
 
     def emit(to, mu):
         own = to == g
@@ -300,8 +306,7 @@
         def _():
             send[to, mu] = block_v[...].astype(BF16)
 
-            via = jnp.where(to > g, g + 1, g - 1)
-            remote(send.at[to, mu], relay_in.at[to, mu], hop_sem, relay_sem.at[to, mu], r, via).start()
+            hop(to, (to, mu), (to, mu))
 
     def block(to, mu):
         at = pl.ds(pl.multiple_of(to * j_dev, j_dev), j_dev)
@@ -310,8 +315,21 @@
     initial = choose(g, [order[0] for order in orders])
 
     make_vectors(first_mu)
-    block(initial, first_mu)
-    emit(initial, first_mu)
+    if chained(G) and G > 1:
+        for half in range(2):
+            rows = pl.ds(half * (j_dev // 2), j_dev // 2)
+            at = pl.ds(pl.multiple_of(initial * j_dev + half * (j_dev // 2), j_dev // 2), j_dev // 2)
+            block_v[rows, :] = jnp.dot(orb_t[at, :], new_v[first_mu], preferred_element_type=F32)
+
+            @pl.when(at_end)
+            def _():
+                send[initial, first_mu, rows, :] = block_v[rows, :].astype(BF16)
+                hop(initial, (initial, first_mu, rows), (initial, first_mu))
+
+        pl.when(jnp.logical_not(at_end))(lambda: emit(initial, first_mu))
+    else:
+        block(initial, first_mu)
+        emit(initial, first_mu)
 
     @pl.loop(1, mu_dev)
     def _(mu):
@@ -319,11 +337,24 @@
         block(initial, mu)
         emit(initial, mu)
 
-    for s in range(1, G):
+    rest = list(range(1, G))
+    paired = rest[-2:] if chained(G) and G > 2 else []
+    for s in rest[: len(rest) - len(paired)]:
         to = choose(g, [order[s] for order in orders])
 
         @pl.loop(0, mu_dev)
         def _(mu):
+            block(to, mu)
+            emit(to, mu)
+
+    if paired:
+        one, two = [choose(g, [order[s] for order in orders]) for s in paired]
+
+        @pl.loop(0, 2 * mu_dev)
+        def _(t):
+            second_one = jnp.where(at_end, t // mu_dev, lax.rem(t, 2))
+            mu = jnp.where(at_end, lax.rem(t, mu_dev), t // 2)
+            to = jnp.where(second_one == 0, one, two)
             block(to, mu)
             emit(to, mu)
 

time: 65 us -> 64.4 us (level)
  no operation moved by 1% of the time
where the time goes in v7:
time: 64.4 us; the launch traced here: 64 us
  Pallas kernels  63.3 us (98%)
  between operations  0.66 us (1%)
    pallas_call x1, Pallas kernels, fused(): pl.pallas_call(functools.partial(fused_kernel, R, G), out_shape=(jax.Shap...  55.6 us
    pallas_call x1, Pallas kernels, orbital_block(): pl.pallas_call(block_kernel, out_shape=(jax.ShapeDtypeStruct((groups, lot...  7.79 us

profile of v7, /device:TPU:9, one launch (start us, length us, event | category | flops | bytes accessed | tf_op | source)
XLA Modules:
  0.0 64.0 jit_solution(6746346929141990272)
XLA Ops:
  0.6 0.0 copy-start
  0.6 55.6 %fused_exchange.1 = (bf16[32,32,256]{2,1,0:T(8,128)(2,1)S(1)}, bf16[4,2560,256]{2,1,0:T(8,128)(2,1)S(1)}) custom-call(s32[1,256]{1,0:T(1,128)} %bitcast.2, bf16[4,2560,256]{2,1,0:T(8,128)(2,1)} %pc_hbm.1, bf16[4,2560,512]{2,1,0:T(8,128)(2,1)} %prev_hbm.1, bf16[256,256]{1,0:T(8,128)(2,1)} %inv_hbm.1, bf16[2560,1024]{1,0:T(8,128)(2,1)} %orb_hbm.1), custom_call_target="tpu_custom_call" | custom-call | tf_op jit(solution)/shard_map/fused_exchange/pallas_call | solution.py:422
  56.2 0.0 copy-done
  56.2 7.8 %orbital_block.1 = (bf16[4,8,1024,256]{3,2,1,0:T(8,128)(2,1)}, bf16[4,2560,256]{2,1,0:T(8,128)(2,1)}) custom-call(bf16[32,32,256]{2,1,0:T(8,128)(2,1)S(1)} %get-tuple-element.6.part_ref, bf16[32,1024]{1,0:T(8,128)(2,1)S(1)} %copy-done, bf16[4,2560,256]{2,1,0:T(8,128)(2,1)S(1)} %get-tuple-element.7.made_ref), custom_call_target="tpu_custom_call" | custom-call | tf_op jit(solution)/shard_map/orbital_block/pallas_call | solution.py:501
Async XLA Ops:
  0.6 55.6 %copy-start = (bf16[32,1024]{1,0:T(8,128)(2,1)S(1)}, bf16[32,1024]{1,0:T(8,128)(2,1)}, u32[]{:S(2)}) copy-start(bf16[32,1024]{1,0:T(8,128)(2,1)} %slab_ref.1) | copy-start | bytes 196612

commit v8 on v7

--- a/solution.py
+++ b/solution.py
@@ -34,7 +34,7 @@
 
 def fused_kernel(
     R, G, piv_hbm, pc_hbm, prev_hbm, inv_hbm, orb_hbm, out_v, new_v,
-    piv_v, inv_v, piv_col, hot_v, picked, buf_x, buf_a, buf_b, buf_c, rows_t, upper_v, prev_v, orb_v, orb_t,
+    piv_v, inv_v, piv_col, within, hot_v, picked, buf_x, buf_a, buf_b, buf_c, rows_t, upper_v, prev_v, orb_v, orb_t,
     block_v, begun, send, relay_in, last, own_out, last_in, own_in,
     rows_send, recv_a, recv_b, recv_c, small_sem, prev_sem, pc_sem, orb_sem,
     hop_sem, relay_sem, last_send, last_recv, own_send, own_recv,
@@ -72,6 +72,9 @@
     greet_rows(0)
     for d in range(1, G):
         greet(r, lax.rem(g + d, G))
+    for h in range(halves):
+        for mu in range(mu_dev):
+            load_prev(h, mu).start()
     if chained(G):
         if G > 1:
             pl.when(g > 0)(lambda: greet_rows(-1))
@@ -82,20 +85,21 @@
             greet_rows(d)
         sides = G - 1
     greetings = (sides + 1) * (R - 1) + G - 1
-    for h in range(halves):
-        for mu in range(mu_dev):
-            load_prev(h, mu).start()
     load_inv.start()
     load_piv.wait()
 
     lanes = piv_col.shape[1]
-    piv_col[...] = jnp.broadcast_to(piv_v[...], (lanes, p)).T
+    turned_piv = jnp.broadcast_to(piv_v[...], (lanes, p)).T
+    lane = lax.broadcasted_iota(jnp.int32, (p, lanes), 1)
+    piv_col[...] = lax.shift_right_arithmetic(turned_piv, lanes.bit_length() - 1)
+    within[...] = jnp.where((turned_piv & (lanes - 1)) == lane, 1.0, 0.0).astype(BF16)
 
     def heat(mu):
         base = (r * mu_dev + mu) * (nu * G) + g * nu
+        tile = (piv_col[...] - base // lanes).astype(F32).astype(BF16)
         for i in range(nu // lanes):
-            at = lax.broadcasted_iota(jnp.int32, (p, lanes), 1) + (base + i * lanes)
-            hot_v[mu, :, i * lanes : (i + 1) * lanes] = jnp.where(piv_col[...] == at, 1.0, 0.0).astype(BF16)
+            here = tile == jnp.full(tile.shape, i, BF16)
+            hot_v[mu, :, i * lanes : (i + 1) * lanes] = jnp.where(here, within[...], jnp.zeros(tile.shape, BF16))
 
     def remote(src, dst, send, recv, row, grp):
         return pltpu.make_async_remote_copy(
@@ -368,13 +372,20 @@
         def _():
             own_in[...] += last_in[slot].astype(F32)
 
+    def finish(slot, when):
+        take(last_in.at[slot], last_recv.at[slot], when)
+
+        @pl.when(when)
+        def _():
+            out_v[...] = (own_in[...] + last_in[slot].astype(F32)).astype(BF16)
+
     inner = jnp.logical_not(at_end)
     others = own_in.at[pl.ds(0, (R - 1) * mu_dev)]
     take(others, own_recv, inner)
     if chained(G):
-        gather(0, inner & (2 * g >= G))
-        gather(1, inner)
-        gather(0, inner & (2 * g < G))
+        for slot, when in ((0, inner & (2 * g < G)), (1, inner & (2 * g >= G))):
+            gather(1 - slot, when)
+            finish(slot, when)
         rounded = last_in.at[0, pl.ds(0, (R - 1) * mu_dev)]
         take(rounded, last_recv.at[0], at_end)
 
@@ -384,9 +395,6 @@
     else:
         for slot in range(G):
             gather(slot, g != slot)
-
-    @pl.when(inner)
-    def _():
         out_v[...] = own_in[...].astype(BF16)
 
     every = pl.ds(0, k_all)
@@ -431,6 +439,7 @@
             pltpu.VMEM((1, p), jnp.int32),
             pltpu.VMEM((p, p), BF16),
             pltpu.VMEM((p, 128), jnp.int32),
+            pltpu.VMEM((p, 128), BF16),
             pltpu.VMEM((mu_dev, p, nu), BF16),
             pltpu.VMEM((p, kh), F32),
             pltpu.VMEM((R, c, k), BF16),

time: 64.4 us -> 64.3 us (level)
  no operation moved by 1% of the time
where the time goes in v8:
time: 64.3 us; the launch traced here: 63.9 us
  Pallas kernels  63.2 us (98%)
  between operations  0.66 us (1%)
    pallas_call x1, Pallas kernels, fused(): pl.pallas_call(functools.partial(fused_kernel, R, G), out_shape=(jax.Shap...  55.4 us
    pallas_call x1, Pallas kernels, orbital_block(): pl.pallas_call(block_kernel, out_shape=(jax.ShapeDtypeStruct((groups, lot...  7.78 us

profile of v8, /device:TPU:9, one launch (start us, length us, event | category | flops | bytes accessed | tf_op | source)
XLA Modules:
  0.0 63.9 jit_solution(9085124664190606147)
XLA Ops:
  0.6 0.0 copy-start
  0.6 55.4 %fused_exchange.1 = (bf16[32,32,256]{2,1,0:T(8,128)(2,1)S(1)}, bf16[4,2560,256]{2,1,0:T(8,128)(2,1)S(1)}) custom-call(s32[1,256]{1,0:T(1,128)} %bitcast.2, bf16[4,2560,256]{2,1,0:T(8,128)(2,1)} %pc_hbm.1, bf16[4,2560,512]{2,1,0:T(8,128)(2,1)} %prev_hbm.1, bf16[256,256]{1,0:T(8,128)(2,1)} %inv_hbm.1, bf16[2560,1024]{1,0:T(8,128)(2,1)} %orb_hbm.1), custom_call_target="tpu_custom_call" | custom-call | tf_op jit(solution)/shard_map/fused_exchange/pallas_call | solution.py:430
  56.1 0.0 copy-done
  56.1 7.8 %orbital_block.1 = (bf16[4,8,1024,256]{3,2,1,0:T(8,128)(2,1)}, bf16[4,2560,256]{2,1,0:T(8,128)(2,1)}) custom-call(bf16[32,32,256]{2,1,0:T(8,128)(2,1)S(1)} %get-tuple-element.6.part_ref, bf16[32,1024]{1,0:T(8,128)(2,1)S(1)} %copy-done, bf16[4,2560,256]{2,1,0:T(8,128)(2,1)S(1)} %get-tuple-element.7.made_ref), custom_call_target="tpu_custom_call" | custom-call | tf_op jit(solution)/shard_map/orbital_block/pallas_call | solution.py:510
Async XLA Ops:
  0.6 55.4 %copy-start = (bf16[32,1024]{1,0:T(8,128)(2,1)S(1)}, bf16[32,1024]{1,0:T(8,128)(2,1)}, u32[]{:S(2)}) copy-start(bf16[32,1024]{1,0:T(8,128)(2,1)} %slab_ref.1) | copy-start | bytes 196612

commit v9 on v8

--- a/solution.py
+++ b/solution.py
@@ -195,7 +195,7 @@
     parted = kh // 2 if kh % 256 == 0 else kh
     pieces = [pl.ds(0, kh)] + [pl.ds(kh + at, parted) for at in range(0, kh, parted)]
     tiles = nu // 256
-    cuts = [0, tiles // 2, tiles * 4 // 5, tiles]
+    cuts = [0, tiles // 2, tiles * 7 // 10, tiles]
     for h in range(halves):
         pick(h)
         if h == 0:

time: 64.3 us -> 64.3 us (level)
  no operation moved by 1% of the time
where the time goes in v9:
time: 64.3 us; the launch traced here: 63.9 us
  Pallas kernels  63.2 us (98%)
  between operations  0.66 us (1%)
    pallas_call x1, Pallas kernels, fused(): pl.pallas_call(functools.partial(fused_kernel, R, G), out_shape=(jax.Shap...  55.4 us
    pallas_call x1, Pallas kernels, orbital_block(): pl.pallas_call(block_kernel, out_shape=(jax.ShapeDtypeStruct((groups, lot...  7.78 us

profile of v9, /device:TPU:9, one launch (start us, length us, event | category | flops | bytes accessed | tf_op | source)
XLA Modules:
  0.0 63.9 jit_solution(10804381905885040730)
XLA Ops:
  0.6 0.0 copy-start
  0.6 55.4 %fused_exchange.1 = (bf16[32,32,256]{2,1,0:T(8,128)(2,1)S(1)}, bf16[4,2560,256]{2,1,0:T(8,128)(2,1)S(1)}) custom-call(s32[1,256]{1,0:T(1,128)} %bitcast.2, bf16[4,2560,256]{2,1,0:T(8,128)(2,1)} %pc_hbm.1, bf16[4,2560,512]{2,1,0:T(8,128)(2,1)} %prev_hbm.1, bf16[256,256]{1,0:T(8,128)(2,1)} %inv_hbm.1, bf16[2560,1024]{1,0:T(8,128)(2,1)} %orb_hbm.1), custom_call_target="tpu_custom_call" | custom-call | tf_op jit(solution)/shard_map/fused_exchange/pallas_call | solution.py:430
  56.1 0.0 copy-done
  56.1 7.8 %orbital_block.1 = (bf16[4,8,1024,256]{3,2,1,0:T(8,128)(2,1)}, bf16[4,2560,256]{2,1,0:T(8,128)(2,1)}) custom-call(bf16[32,32,256]{2,1,0:T(8,128)(2,1)S(1)} %get-tuple-element.6.part_ref, bf16[32,1024]{1,0:T(8,128)(2,1)S(1)} %copy-done, bf16[4,2560,256]{2,1,0:T(8,128)(2,1)S(1)} %get-tuple-element.7.made_ref), custom_call_target="tpu_custom_call" | custom-call | tf_op jit(solution)/shard_map/orbital_block/pallas_call | solution.py:510
Async XLA Ops:
  0.6 55.4 %copy-start = (bf16[32,1024]{1,0:T(8,128)(2,1)S(1)}, bf16[32,1024]{1,0:T(8,128)(2,1)}, u32[]{:S(2)}) copy-start(bf16[32,1024]{1,0:T(8,128)(2,1)} %slab_ref.1) | copy-start | bytes 196612
